TPU v7x, 256 devices: a whole 4x4x8 slice. The times are simulated.
256 devices in a mesh: region: 16 (over z, core), feat: 16 (over y, x).
Axes of the slice: x: 4, y: 4, z: 8, core: 2. Of those that a mesh axis runs over, the one named last changes fastest.
Arguments:
- node_lat: bfloat16 [6144, 512], P(('region', 'feat')), may hold values from -6 to 6
- edge_lat: bfloat16 [49152, 512], P(('region', 'feat')), may hold values from -6 to 6
- receiver_row: int32 [49152], P('region'), may hold values from 0 to 383
- sender_slot: int32 [49152], P('region'), may hold values from 0 to 639, as said below
- send_rows: int32 [16, 16, 16], P('region'), may hold values from 0 to 383
- w_edge_in: bfloat16 [3, 512, 512], P(None, 'feat'), may hold values from -0.15625 to 0.15625
- w_edge_out: bfloat16 [512, 512], P('feat'), may hold values from -0.25 to 0.25
- w_node_in: bfloat16 [2, 512, 512], P(None, 'feat'), may hold values from -0.1875 to 0.1875
- w_node_out: bfloat16 [512, 512], P('feat'), may hold values from -0.25 to 0.25
- edge_gain: float32 [512], P('feat'), may hold values from 0.1 to 1.9
- node_gain: float32 [512], P('feat'), may hold values from 0.1 to 1.9
- node_cot: bfloat16 [6144, 512], P(('region', 'feat')), may hold values from -6 to 6
- edge_cot: bfloat16 [49152, 512], P(('region', 'feat')), may hold values from -6 to 6
Outputs:
- node_new: bfloat16 [6144, 512], P(('region', 'feat'))
- edge_new: bfloat16 [49152, 512], P(('region', 'feat'))
- node_grad: float32 [6144, 512], P(('region', 'feat'))
- edge_grad: float32 [49152, 512], P(('region', 'feat'))
- grad_edge_in: float32 [3, 512, 512], P(None, 'feat')
- grad_edge_out: float32 [512, 512], P('feat')
- grad_node_in: float32 [2, 512, 512], P(None, 'feat')
- grad_node_out: float32 [512, 512], P('feat')
Inputs may be any that keep to these rules, and one draw needn't show every extreme that they name: `receiver_row`: edge e lies in region e // 3072; its receiver is that row of the region's 384 nodes. `sender_slot`: A value below 384 is a row of the edge's own region; a value 384 + p * 16 + s names the node that region p lists in slot s for the edge's region, and p is never the edge's own region. send_rows[p, r, s] is a row of region p's 384 nodes.
All inputs are finite; a program needn't handle non-finite values.
Results may differ from a plain program's by a relative error of at most 0.02.
Values may be sent and summed in bfloat16 or wider, within the bound.
A program may use at most 64 MiB of HBM per device.

v0:
```python
import jax
import jax.numpy as jnp
from jax import lax
from jax.sharding import PartitionSpec as P

EPSILON = 1e-05


def in_order(blocks, dim):
    blocks = jnp.moveaxis(blocks, 0, dim)
    dims = blocks.shape
    return blocks.reshape(*dims[:dim], dims[dim] * dims[dim + 1], *dims[dim + 2 :])


def copy_for_each(array, axis):
    length = lax.axis_size(axis)
    return lax.all_to_all(
        jnp.broadcast_to(array[None], (length, *array.shape)), axis, 0, 0, tiled=True
    )


def gather_directly(array, axis, dim):
    return in_order(copy_for_each(array, axis), dim)


def cut_along(array, dim, length):
    dims = array.shape
    blocks = array.reshape(*dims[:dim], length, dims[dim] // length, *dims[dim + 1 :])
    return jnp.moveaxis(blocks, dim, 0)


def sum_at_owner(array, axis, dim):
    blocks = cut_along(array, dim, lax.axis_size(axis))
    arrived = lax.all_to_all(blocks, axis, split_axis=0, concat_axis=0, tiled=True)
    return arrived.astype(jnp.float32).sum(axis=0)


def side_by_side(arrays, axis, dim, along):
    both = jnp.concatenate(arrays, axis=along)
    whole, at, finished = (lax.all_gather(both, axis, axis=dim, tiled=True), 0, [])
    for a in arrays:
        finished.append(lax.slice_in_dim(whole, at, at + a.shape[along], axis=along))
        at += a.shape[along]
    return tuple(finished)


def over_pieces(array, axis):
    return lax.all_gather(array, axis).astype(jnp.float32).sum(0)


def apply_swish(values):
    return values * jax.nn.sigmoid(values)


def swish_slope(values):
    sigmoid_value = jax.nn.sigmoid(values)
    return sigmoid_value * (1.0 + values * (1.0 - sigmoid_value))


def layer_norm(values, gain_values, breadth):
    sums = jnp.sum(values, axis=1)
    squares = jnp.sum(values * values, axis=1)
    average = sums[:, None] / breadth
    variance = squares[:, None] / breadth - average * average
    inverse = lax.rsqrt(variance + EPSILON)
    normed = (values - average) * inverse
    return (normed, inverse, normed * gain_values)


def layer_norm_back(cotangent, normed, inverse, gain_values, breadth):
    scaled = cotangent * gain_values
    first_sum = jnp.sum(scaled, axis=1)
    second_sum = jnp.sum(scaled * normed, axis=1)
    return (
        inverse * (scaled - first_sum[:, None] / breadth - normed * (second_sum[:, None] / breadth))
    ).astype(jnp.bfloat16)


def matmul_back(first_operand, second_operand):
    return lax.dot_general(
        first_operand, second_operand, (((1,), (1,)), ((), ())), preferred_element_type=jnp.float32
    )


def transposed(first_operand, second_operand):
    return lax.dot_general(
        first_operand, second_operand, (((0,), (0,)), ((), ())), preferred_element_type=jnp.float32
    )


def split_parts(values):
    upper_part = lax.optimization_barrier(values.astype(jnp.bfloat16))
    lower_part = (values - upper_part.astype(jnp.float32)).astype(jnp.bfloat16)
    return (upper_part, lower_part)


def shards(
    node_lat,
    edge_lat,
    receiver_row,
    sender_slot,
    send_rows,
    w_edge_in,
    w_edge_out,
    w_node_in,
    w_node_out,
    edge_gain,
    node_gain,
    node_cot,
    edge_cot,
):
    node_latent_rows = node_lat
    edge_latent_rows = edge_lat
    node_cot_rows = node_cot
    edge_cot_rows = edge_cot
    node_lat, edge_lat, node_cot, edge_cot = (
        lax.all_to_all(node_latent_rows, "feat", split_axis=1, concat_axis=0, tiled=True),
        lax.all_to_all(edge_latent_rows, "feat", split_axis=1, concat_axis=0, tiled=True),
        lax.all_to_all(node_cot_rows, "feat", split_axis=1, concat_axis=0, tiled=True),
        lax.all_to_all(edge_cot_rows, "feat", split_axis=1, concat_axis=0, tiled=True),
    )
    breadth = w_edge_out.shape[1]
    portion = w_edge_out.shape[0]
    node_count = node_lat.shape[0]
    edge_count = edge_lat.shape[0]
    feat_count = lax.axis_size("feat")
    feat_here = lax.axis_index("feat")
    offset = feat_here * portion
    stacked = jnp.concatenate([w_edge_in, w_edge_out[None], w_node_in, w_node_out[None]], axis=0)
    send_list = send_rows[0]
    outgoing = node_lat[send_list]
    incoming = lax.all_to_all(outgoing, "region", split_axis=0, concat_axis=0, tiled=True)
    lookup_table = jnp.concatenate([node_lat, incoming.reshape(-1, portion)], axis=0)
    senders = lookup_table[sender_slot]
    node_ids = jnp.arange(node_count, dtype=jnp.int32)
    incidence = (node_ids[:, None] == receiver_row[None, :]).astype(jnp.bfloat16)
    edge_share = edge_count // feat_count
    full_weights = lax.all_gather(stacked, "feat", axis=1, tiled=True)
    full_gains = gather_directly(jnp.stack([edge_gain, node_gain], axis=0), "feat", 1)
    lookup_full = gather_directly(lookup_table, "feat", 1)
    local_receivers = lax.dynamic_slice_in_dim(receiver_row, feat_here * edge_share, edge_share)
    local_senders = lax.dynamic_slice_in_dim(sender_slot, feat_here * edge_share, edge_share)
    sender_rows = lookup_full[local_senders]
    receiver_rows = lookup_full[local_receivers]
    pre_hidden_rows = (
        jnp.dot(edge_latent_rows, full_weights[0], preferred_element_type=jnp.float32)
        + jnp.dot(sender_rows, full_weights[1], preferred_element_type=jnp.float32)
        + jnp.dot(receiver_rows, full_weights[2], preferred_element_type=jnp.float32)
    )
    hidden_rows = apply_swish(pre_hidden_rows).astype(jnp.bfloat16)
    edge_mix_rows = jnp.dot(hidden_rows, full_weights[3], preferred_element_type=jnp.float32)
    edge_normed_rows, edge_inverse_rows, edge_update_rows = layer_norm(
        edge_mix_rows, full_gains[0], breadth
    )
    edge_new_rows = (edge_latent_rows.astype(jnp.float32) + edge_update_rows).astype(jnp.bfloat16)
    row_incidence = (node_ids[:, None] == local_receivers[None, :]).astype(jnp.bfloat16)
    pooled_rows = sum_at_owner(
        jnp.dot(row_incidence, edge_new_rows, preferred_element_type=jnp.float32).astype(
            jnp.bfloat16
        ),
        "feat",
        0,
    ).astype(jnp.bfloat16)
    node_pre_rows = jnp.dot(
        node_latent_rows, full_weights[4], preferred_element_type=jnp.float32
    ) + jnp.dot(pooled_rows, full_weights[5], preferred_element_type=jnp.float32)
    node_hidden_rows = apply_swish(node_pre_rows).astype(jnp.bfloat16)
    node_mix_rows = jnp.dot(node_hidden_rows, full_weights[6], preferred_element_type=jnp.float32)
    node_normed_rows, node_inverse_rows, node_update_rows = layer_norm(
        node_mix_rows, full_gains[1], breadth
    )
    node_new_rows = (node_latent_rows.astype(jnp.float32) + node_update_rows).astype(jnp.bfloat16)
    node_mix_grad_rows = layer_norm_back(
        node_cot_rows.astype(jnp.float32),
        node_normed_rows,
        node_inverse_rows,
        full_gains[1],
        breadth,
    )
    node_pre_grad_rows = (
        matmul_back(node_mix_grad_rows, full_weights[6]) * swish_slope(node_pre_rows)
    ).astype(jnp.bfloat16)
    node_pre_wide, node_mix_wide = side_by_side(
        (node_pre_grad_rows, node_mix_grad_rows), "feat", 0, 1
    )
    pooled_full = matmul_back(node_pre_wide, full_weights[5])
    edge_total_rows = edge_cot_rows.astype(jnp.float32) + pooled_full[local_receivers]
    edge_mix_grad_rows = layer_norm_back(
        edge_total_rows, edge_normed_rows, edge_inverse_rows, full_gains[0], breadth
    )
    pre_grad_rows = (
        matmul_back(edge_mix_grad_rows, full_weights[3]) * swish_slope(pre_hidden_rows)
    ).astype(jnp.bfloat16)
    pre_wide, edge_mix_wide = side_by_side((pre_grad_rows, edge_mix_grad_rows), "feat", 0, 1)
    pooled_grad = lax.dynamic_slice_in_dim(pooled_full, offset, portion, 1)
    edge_total = edge_cot.astype(jnp.float32) + pooled_grad[receiver_row]
    node_hidden, pooled, hidden = (
        lax.all_to_all(node_hidden_rows, "feat", split_axis=1, concat_axis=0, tiled=True),
        lax.all_to_all(pooled_rows, "feat", split_axis=1, concat_axis=0, tiled=True),
        lax.all_to_all(hidden_rows, "feat", split_axis=1, concat_axis=0, tiled=True),
    )
    grad_node_second_layer = transposed(node_hidden, node_mix_wide)
    node_direct = matmul_back(node_pre_wide, w_node_in[0])
    grad_node_latent = transposed(node_lat, node_pre_wide)
    grad_node_pooled = transposed(pooled, node_pre_wide)
    grad_edge_second_layer = transposed(hidden, edge_mix_wide)
    edge_grad = edge_total + matmul_back(pre_wide, w_edge_in[0])
    sender_grad = matmul_back(pre_wide, w_edge_in[1])
    grad_edge_latent = transposed(edge_lat, pre_wide)
    grad_edge_sender = transposed(senders, pre_wide)
    summed = jnp.dot(incidence, pre_wide, preferred_element_type=jnp.float32)
    upper_part, lower_part = split_parts(summed)
    receiver_grad = matmul_back(upper_part, w_edge_in[2]) + matmul_back(lower_part, w_edge_in[2])
    grad_edge_receiver = transposed(node_lat, upper_part) + transposed(node_lat, lower_part)
    table_grad = jax.ops.segment_sum(sender_grad, sender_slot, num_segments=lookup_table.shape[0])
    remote_grad = table_grad[node_count:].reshape(send_list.shape[0], send_list.shape[1], portion)
    returned = lax.all_to_all(
        remote_grad.astype(jnp.bfloat16), "region", split_axis=0, concat_axis=0, tiled=True
    ).astype(remote_grad.dtype)
    node_grad = (
        node_cot.astype(jnp.float32)
        + node_direct
        + receiver_grad
        + table_grad[:node_count]
        + jax.ops.segment_sum(
            returned.reshape(-1, portion), send_list.reshape(-1), num_segments=node_count
        )
    )
    node_grad_out, edge_grad_out = (
        lax.all_to_all(
            node_grad.astype(jnp.bfloat16), "feat", split_axis=0, concat_axis=1, tiled=True
        ).astype(node_grad.dtype),
        lax.all_to_all(
            edge_grad.astype(jnp.bfloat16), "feat", split_axis=0, concat_axis=1, tiled=True
        ).astype(edge_grad.dtype),
    )
    summed_grads = (
        over_pieces(
            jnp.stack([grad_edge_latent, grad_edge_sender, grad_edge_receiver], axis=0).astype(
                jnp.bfloat16
            ),
            "region",
        ).astype(jnp.float32),
        over_pieces(grad_edge_second_layer.astype(jnp.bfloat16), "region").astype(jnp.float32),
        over_pieces(
            jnp.stack([grad_node_latent, grad_node_pooled], axis=0).astype(jnp.bfloat16), "region"
        ).astype(jnp.float32),
        over_pieces(grad_node_second_layer.astype(jnp.bfloat16), "region").astype(jnp.float32),
    )
    edge_norm = 1.0 / jnp.sqrt(jnp.float32(edge_count * lax.axis_size("region")))
    node_norm = 1.0 / jnp.sqrt(jnp.float32(node_count * lax.axis_size("region")))
    return (
        node_new_rows,
        edge_new_rows,
        node_grad_out,
        edge_grad_out,
        summed_grads[0] * edge_norm,
        summed_grads[1] * edge_norm,
        summed_grads[2] * node_norm,
        summed_grads[3] * node_norm,
    )


def solution(mesh):
    in_specs = (
        P(("region", "feat"), None),
        P(("region", "feat"), None),
        P("region"),
        P("region"),
        P("region", None, None),
        P(None, "feat", None),
        P("feat", None),
        P(None, "feat", None),
        P("feat", None),
        P("feat"),
        P("feat"),
        P(("region", "feat"), None),
        P(("region", "feat"), None),
    )
    out_specs = (
        P(("region", "feat"), None),
        P(("region", "feat"), None),
        P(("region", "feat"), None),
        P(("region", "feat"), None),
        P(None, "feat", None),
        P("feat", None),
        P(None, "feat", None),
        P("feat", None),
    )
    return jax.shard_map(shards, mesh=mesh, in_specs=in_specs, out_specs=out_specs, check_vma=False)
```

profile of v0, /device:TPU:1, one launch (start us, length us, event | category | flops | bytes accessed | tf_op | source)
XLA Modules:
  0.0 353.3 jit_solution(5768868887525092924)
XLA Ops:
  10.6 7.6 %all-to-all-start = ((bf16[16,2,384]{2,1,0:T(2,128)(2,1)}), bf16[16,2,384]{2,1,0:T(2,128)(2,1)S(1)}, u32[]{:S(2)}, u32[]{:S(2)}) async-start(bf16[16,2,384]{2,1,0:T(2,128)(2,1)} %reshape.341), calls=%async_computation | async-start | bytes 49152 | tf_op jit(solution)/shard_map/all_to_all | solution.py:117
  19.7 4.9 %all-to-all-done = bf16[16,2,384]{2,1,0:T(2,128)(2,1)S(1)} async-done(((bf16[16,2,384]{2,1,0:T(2,128)(2,1)}), bf16[16,2,384]{2,1,0:T(2,128)(2,1)S(1)}, u32[]{:S(2)}, u32[]{:S(2)}) %all-to-all-start) | async-done | bytes 24608 | tf_op jit(solution)/shard_map/all_to_all | solution.py:117
  26.3 10.6 %all-to-all-start.1 = ((bf16[16,2,256]{2,1,0:T(2,128)(2,1)}), bf16[16,2,256]{2,1,0:T(2,128)(2,1)S(1)}, u32[]{:S(2)}, u32[]{:S(2)}) async-start(bf16[16,2,256]{2,1,0:T(2,128)(2,1)} %reshape.343), calls=%async_computation.1 | async-start | bytes 32768 | tf_op jit(solution)/shard_map/all_to_all | solution.py:132
  37.6 6.7 %all-to-all-done.1 = bf16[16,2,256]{2,1,0:T(2,128)(2,1)S(1)} async-done(((bf16[16,2,256]{2,1,0:T(2,128)(2,1)}), bf16[16,2,256]{2,1,0:T(2,128)(2,1)S(1)}, u32[]{:S(2)}, u32[]{:S(2)}) %all-to-all-start.1) | async-done | bytes 16416 | tf_op jit(solution)/shard_map/all_to_all | solution.py:132
  48.6 6.1 %all-to-all-done.3 = f32[16,2,32]{2,1,0:T(2,128)S(1)} async-done(((f32[16,2,32]{2,1,0:T(2,128)}), f32[16,2,32]{2,1,0:T(2,128)S(1)}, u32[]{:S(2)}, u32[]{:S(2)}) %all-to-all-start.3) | async-done | bytes 4128 | tf_op jit(solution)/shard_map/all_to_all | solution.py:17
  59.6 17.6 %all-to-all-done.2 = bf16[16,640,32]{1,2,0:T(8,128)(2,1)S(1)} async-done(((bf16[16,640,32]{1,2,0:T(8,128)(2,1)}), bf16[16,640,32]{1,2,0:T(8,128)(2,1)S(1)}, u32[]{:S(2)}, u32[]{:S(2)}) %all-to-all-start.2) | async-done | bytes 655392 | tf_op jit(solution)/shard_map/all_to_all | solution.py:17
  91.7 7.5 %all-to-all-done.4 = bf16[16,24,512]{2,1,0:T(8,128)(2,1)S(1)} async-done(((bf16[16,24,512]{2,1,0:T(8,128)(2,1)}), bf16[16,24,512]{2,1,0:T(8,128)(2,1)S(1)}, u32[]{:S(2)}, u32[]{:S(2)}) %all-to-all-start.4) | async-done | bytes 393248 | tf_op jit(solution)/shard_map/all_to_all | solution.py:34
  104.1 17.4 %all_gather.30 = bf16[384,1024]{1,0:T(8,128)(2,1)S(1)} all-gather(bf16[24,1024]{1,0:T(8,128)(2,1)S(1)} %pad_maximum_fusion.5), channel_id=1, replica_groups=mesh['region'=16,'feat'=16] {'feat'}, dimensions={0}, use_global_device_ids=true | all-gather | bytes 835584 | tf_op jit(solution)/shard_map/all_gather | solution.py:40
  127.6 4.6 %all-to-all-start.5 = ((bf16[16,2,384]{2,1,0:T(2,128)(2,1)}), bf16[16,2,384]{2,1,0:T(2,128)(2,1)S(1)}, u32[]{:S(2)}, u32[]{:S(2)}) async-start(bf16[16,2,384]{2,1,0:T(2,128)(2,1)} %reshape.345), calls=%async_computation.5 | async-start | bytes 49152 | tf_op jit(solution)/shard_map/all_to_all | solution.py:119
  142.3 8.5 %all-to-all-done.10 = bf16[192,16,32]{0,2,1:T(8,128)(2,1)S(1)} async-done(((bf16[192,16,32]{0,2,1:T(8,128)(2,1)}), bf16[192,16,32]{0,2,1:T(8,128)(2,1)S(1)}, u32[]{:S(2)}, u32[]{:S(2)}) %all-to-all-start.10) | async-done | bytes 196640 | tf_op jit(solution)/shard_map/all_to_all | solution.py:118
  155.1 11.5 %gather_fusion.5 = bf16[3072,32]{1,0:T(8,128)(2,1)} fusion(bf16[640,32]{1,0:T(8,128)(2,1)S(1)} %pad_maximum_fusion.2, s32[3072]{0:T(1024)S(1)} %fusion.65), kind=kCustom, calls=%fused_computation.5 | custom fusion | bytes 405504 | tf_op jit(solution)/shard_map/gather | solution.py:134
  168.6 6.6 %all-to-all-start.11 = ((bf16[192,16,32]{0,2,1:T(8,128)(2,1)}), bf16[192,16,32]{0,2,1:T(8,128)(2,1)S(1)}, u32[]{:S(2)}, u32[]{:S(2)}) async-start(bf16[192,16,32]{0,2,1:T(8,128)(2,1)} %bitcast.45), calls=%async_computation.11 | async-start | bytes 524288 | tf_op jit(solution)/shard_map/all_to_all | solution.py:200
  175.7 9.9 %all-to-all-done.11 = bf16[192,16,32]{0,2,1:T(8,128)(2,1)S(1)} async-done(((bf16[192,16,32]{0,2,1:T(8,128)(2,1)}), bf16[192,16,32]{0,2,1:T(8,128)(2,1)S(1)}, u32[]{:S(2)}, u32[]{:S(2)}) %all-to-all-start.11) | async-done | bytes 196640 | tf_op jit(solution)/shard_map/all_to_all | solution.py:200
  192.6 8.1 %gather_fusion.4 = f32[3072,32]{1,0:T(8,128)S(1)} fusion(f32[384,32]{1,0:T(8,128)S(1)} %constant_dynamic-slice_fusion, s32[3072]{0:T(1024)S(1)} %fusion.64), kind=kCustom, calls=%fused_computation.4 | custom fusion | bytes 798720 | tf_op jit(solution)/shard_map/gather | solution.py:196
  201.9 6.6 %all-to-all-start.13 = ((bf16[16,2,384]{2,1,0:T(2,128)(2,1)}), bf16[16,2,384]{2,1,0:T(2,128)(2,1)S(1)}, u32[]{:S(2)}, u32[]{:S(2)}) async-start(bf16[16,2,384]{2,1,0:T(2,128)(2,1)} %reshape.353), calls=%async_computation.13 | async-start | bytes 49152 | tf_op jit(solution)/shard_map/all_to_all | solution.py:198
  209.6 5.4 %all-to-all-done.13 = bf16[16,2,384]{2,1,0:T(2,128)(2,1)S(1)} async-done(((bf16[16,2,384]{2,1,0:T(2,128)(2,1)}), bf16[16,2,384]{2,1,0:T(2,128)(2,1)S(1)}, u32[]{:S(2)}, u32[]{:S(2)}) %all-to-all-start.13) | async-done | bytes 24608 | tf_op jit(solution)/shard_map/all_to_all | solution.py:198
  215.2 33.1 %all-gather.1 = bf16[512,512]{1,0:T(8,128)(2,1)S(1)} all-gather(bf16[32,512]{1,0:T(8,128)(2,1)S(1)} %convolution_convert_fusion.1), channel_id=3, replica_groups=mesh['region'=16,'feat'=16] {'region'}, dimensions={0}, use_global_device_ids=true | all-gather | bytes 557056 | tf_op jit(solution)/shard_map/all_gather | solution.py:48
  255.2 7.1 %all-gather.13.cloned.1.call-done = bf16[16,2,32,512]{3,2,1,0:T(8,128)(2,1)} async-done(((bf16[1,2,32,512]{3,2,1,0:T(8,128)(2,1)}), bf16[16,2,32,512]{3,2,1,0:T(8,128)(2,1)}) %all-gather.13.cloned.1.call-update) | async-done | bytes 1048592 | tf_op jit(solution)/shard_map/all_gather | solution.py:48
  268.3 17.4 %scatter_custom_fusion = f32[640,32]{1,0:T(8,128)S(1)} fusion(s32[3072]{0:T(1024)} %param.16, f32[3072,32]{1,0:T(8,128)} %fusion.10, f32[]{:T(128)} %constant.22.clone.1), kind=kCustom, calls=%fused_computation.86 | custom fusion | flops 98304 | bytes 82432 | tf_op jit(solution)/shard_map/scatter-add | solution.py:215
  286.6 4.6 %all-to-all-start.6 = ((bf16[16,2,256]{2,1,0:T(2,128)(2,1)}), bf16[16,2,256]{2,1,0:T(2,128)(2,1)S(1)}, u32[]{:S(2)}, u32[]{:S(2)}) async-start(bf16[16,2,256]{2,1,0:T(2,128)(2,1)} %reshape.347), calls=%async_computation.6 | async-start | bytes 32768 | tf_op jit(solution)/shard_map/all_to_all | solution.py:217
  294.0 18.6 %all-gather = bf16[512,512]{1,0:T(8,128)(2,1)S(1)} all-gather(bf16[32,512]{1,0:T(8,128)(2,1)S(1)} %fusion.18), channel_id=2, replica_groups=mesh['region'=16,'feat'=16] {'region'}, dimensions={0}, use_global_device_ids=true | all-gather | bytes 557056 | tf_op jit(solution)/shard_map/all_gather | solution.py:48
  319.3 6.6 %all-to-all-start.7 = ((bf16[16,2,384]{2,1,0:T(2,128)(2,1)}), bf16[16,2,384]{2,1,0:T(2,128)(2,1)S(1)}, u32[]{:S(2)}, u32[]{:S(2)}) async-start(bf16[16,2,384]{2,1,0:T(2,128)(2,1)} %reshape.349), calls=%async_computation.7 | async-start | bytes 49152 | tf_op jit(solution)/shard_map/all_to_all | solution.py:230
  327.7 4.7 %all-to-all-done.7 = bf16[16,2,384]{2,1,0:T(2,128)(2,1)S(1)} async-done(((bf16[16,2,384]{2,1,0:T(2,128)(2,1)}), bf16[16,2,384]{2,1,0:T(2,128)(2,1)S(1)}, u32[]{:S(2)}, u32[]{:S(2)}) %all-to-all-start.7) | async-done | bytes 24608 | tf_op jit(solution)/shard_map/all_to_all | solution.py:230
  336.9 6.6 %all-to-all-done.9 = bf16[16,192,32]{1,2,0:T(8,128)(2,1)S(1)} async-done(((bf16[16,192,32]{1,2,0:T(8,128)(2,1)}), bf16[16,192,32]{1,2,0:T(8,128)(2,1)S(1)}, u32[]{:S(2)}, u32[]{:S(2)}) %all-to-all-start.9) | async-done | bytes 196640 | tf_op jit(solution)/shard_map/all_to_all | solution.py:233
  (178 shorter events, 100.7 us)
Async XLA Ops:
  7.2 52.2 %copy-start.15 = (s32[3072]{0:T(1024)S(1)}, s32[3072]{0:T(1024)}, u32[]{:S(2)}) copy-start(s32[3072]{0:T(1024)} %param.16) | copy-start | bytes 36868
  7.2 72.2 %all-gather.7.cloned.1.call-start = ((), (), s32[]{:S(2)}) async-start(), calls=%async_computation.14 | async-start | bytes 3899392 | tf_op jit(solution)/shard_map/all_gather | solution.py:138
  10.6 14.0 %all-to-all-start = ((bf16[16,2,384]{2,1,0:T(2,128)(2,1)}), bf16[16,2,384]{2,1,0:T(2,128)(2,1)S(1)}, u32[]{:S(2)}, u32[]{:S(2)}) async-start(bf16[16,2,384]{2,1,0:T(2,128)(2,1)} %reshape.341), calls=%async_computation | async-start | bytes 49152 | tf_op jit(solution)/shard_map/all_to_all | solution.py:117
  26.3 17.9 %all-to-all-start.1 = ((bf16[16,2,256]{2,1,0:T(2,128)(2,1)}), bf16[16,2,256]{2,1,0:T(2,128)(2,1)S(1)}, u32[]{:S(2)}, u32[]{:S(2)}) async-start(bf16[16,2,256]{2,1,0:T(2,128)(2,1)} %reshape.343), calls=%async_computation.1 | async-start | bytes 32768 | tf_op jit(solution)/shard_map/all_to_all | solution.py:132
  44.8 9.9 %all-to-all-start.3 = ((f32[16,2,32]{2,1,0:T(2,128)}), f32[16,2,32]{2,1,0:T(2,128)S(1)}, u32[]{:S(2)}, u32[]{:S(2)}) async-start(f32[16,2,32]{2,1,0:T(2,128)} %broadcast_in_dim.27), calls=%async_computation.3 | async-start | bytes 32768 | tf_op jit(solution)/shard_map/all_to_all | solution.py:17
  55.6 25.1 %copy-start.2 = (bf16[192,512]{1,0:T(8,128)(2,1)S(1)}, bf16[192,512]{1,0:T(8,128)(2,1)}, u32[]{:S(2)}) copy-start(bf16[192,512]{1,0:T(8,128)(2,1)} %param.14) | copy-start | bytes 589828
  55.6 21.5 %all-to-all-start.2 = ((bf16[16,640,32]{1,2,0:T(8,128)(2,1)}), bf16[16,640,32]{1,2,0:T(8,128)(2,1)S(1)}, u32[]{:S(2)}, u32[]{:S(2)}) async-start(bf16[16,640,32]{1,2,0:T(8,128)(2,1)} %broadcast_in_dim.24), calls=%async_computation.2 | async-start | bytes 1310720 | tf_op jit(solution)/shard_map/all_to_all | solution.py:17
  85.8 37.2 %copy-start.4 = (bf16[192,512]{1,0:T(8,128)(2,1)}, bf16[192,512]{1,0:T(8,128)(2,1)S(1)}, u32[]{:S(2)}) copy-start(bf16[192,512]{1,0:T(8,128)(2,1)S(1)} %add_convert_fusion) | copy-start | bytes 589828
  86.8 12.4 %all-to-all-start.4 = ((bf16[16,24,512]{2,1,0:T(8,128)(2,1)}), bf16[16,24,512]{2,1,0:T(8,128)(2,1)S(1)}, u32[]{:S(2)}, u32[]{:S(2)}) async-start(bf16[16,24,512]{2,1,0:T(8,128)(2,1)} %bitcast.21), calls=%async_computation.4 | async-start | bytes 786432 | tf_op jit(solution)/shard_map/all_to_all | solution.py:34
  90.4 158.0 %all-gather.9.cloned.1.call-start = ((), (), s32[]{:S(2)}) async-start(), calls=%async_computation.15 | async-start | bytes 6684672 | tf_op jit(solution)/shard_map/all_gather | solution.py:40
  127.6 11.1 %all-to-all-start.5 = ((bf16[16,2,384]{2,1,0:T(2,128)(2,1)}), bf16[16,2,384]{2,1,0:T(2,128)(2,1)S(1)}, u32[]{:S(2)}, u32[]{:S(2)}) async-start(bf16[16,2,384]{2,1,0:T(2,128)(2,1)} %reshape.345), calls=%async_computation.5 | async-start | bytes 49152 | tf_op jit(solution)/shard_map/all_to_all | solution.py:119
  138.6 12.2 %all-to-all-start.10 = ((bf16[192,16,32]{0,2,1:T(8,128)(2,1)}), bf16[192,16,32]{0,2,1:T(8,128)(2,1)S(1)}, u32[]{:S(2)}, u32[]{:S(2)}) async-start(bf16[192,16,32]{0,2,1:T(8,128)(2,1)} %bitcast.38), calls=%async_computation.10 | async-start | bytes 524288 | tf_op jit(solution)/shard_map/all_to_all | solution.py:118
  150.8 17.7 %all-to-all-start.8 = ((bf16[192,16,32]{0,2,1:T(8,128)(2,1)}), bf16[192,16,32]{0,2,1:T(8,128)(2,1)S(1)}, u32[]{:S(2)}, u32[]{:S(2)}) async-start(bf16[192,16,32]{0,2,1:T(8,128)(2,1)} %bitcast.33), calls=%async_computation.8 | async-start | bytes 524288 | tf_op jit(solution)/shard_map/all_to_all | solution.py:120
  166.6 24.6 %copy-start.10 = (bf16[2,32,512]{2,1,0:T(8,128)(2,1)S(1)}, bf16[2,32,512]{2,1,0:T(8,128)(2,1)}, u32[]{:S(2)}) copy-start(bf16[2,32,512]{2,1,0:T(8,128)(2,1)} %param.20) | copy-start | bytes 196612
  166.6 24.6 %copy-start.11 = (f32[384,32]{0,1:T(8,128)S(1)}, f32[384,32]{0,1:T(8,128)}, u32[]{:S(2)}) copy-start(f32[384,32]{0,1:T(8,128)} %copy.171) | copy-start | bytes 147460
  168.6 17.1 %all-to-all-start.11 = ((bf16[192,16,32]{0,2,1:T(8,128)(2,1)}), bf16[192,16,32]{0,2,1:T(8,128)(2,1)S(1)}, u32[]{:S(2)}, u32[]{:S(2)}) async-start(bf16[192,16,32]{0,2,1:T(8,128)(2,1)} %bitcast.45), calls=%async_computation.11 | async-start | bytes 524288 | tf_op jit(solution)/shard_map/all_to_all | solution.py:200
  186.9 15.0 %all-to-all-start.12 = ((bf16[16,2,384]{2,1,0:T(2,128)(2,1)}), bf16[16,2,384]{2,1,0:T(2,128)(2,1)S(1)}, u32[]{:S(2)}, u32[]{:S(2)}) async-start(bf16[16,2,384]{2,1,0:T(2,128)(2,1)} %reshape.351), calls=%async_computation.12 | async-start | bytes 49152 | tf_op jit(solution)/shard_map/all_to_all | solution.py:199
  201.9 13.0 %all-to-all-start.13 = ((bf16[16,2,384]{2,1,0:T(2,128)(2,1)}), bf16[16,2,384]{2,1,0:T(2,128)(2,1)S(1)}, u32[]{:S(2)}, u32[]{:S(2)}) async-start(bf16[16,2,384]{2,1,0:T(2,128)(2,1)} %reshape.353), calls=%async_computation.13 | async-start | bytes 49152 | tf_op jit(solution)/shard_map/all_to_all | solution.py:198
  208.5 53.7 %all-gather.13.cloned.1.call-start = ((), (), s32[]{:S(2)}) async-start(), calls=%async_computation.17 | async-start | bytes 1114112 | tf_op jit(solution)/shard_map/all_gather | solution.py:48
  209.5 134.9 %all-gather.11.cloned.1.call-start = ((), (), s32[]{:S(2)}) async-start(), calls=%async_computation.16 | async-start | bytes 1671168 | tf_op jit(solution)/shard_map/all_gather | solution.py:48
  268.3 44.6 %copy-start.5 = (f32[3072,32]{0,1:T(8,128)S(1)}, f32[3072,32]{0,1:T(8,128)}, u32[]{:S(2)}) copy-start(f32[3072,32]{0,1:T(8,128)} %copy.159) | copy-start | bytes 1179652
  286.6 29.5 %all-to-all-start.6 = ((bf16[16,2,256]{2,1,0:T(2,128)(2,1)}), bf16[16,2,256]{2,1,0:T(2,128)(2,1)S(1)}, u32[]{:S(2)}, u32[]{:S(2)}) async-start(bf16[16,2,256]{2,1,0:T(2,128)(2,1)} %reshape.347), calls=%async_computation.6 | async-start | bytes 32768 | tf_op jit(solution)/shard_map/all_to_all | solution.py:217
  319.3 13.1 %all-to-all-start.7 = ((bf16[16,2,384]{2,1,0:T(2,128)(2,1)}), bf16[16,2,384]{2,1,0:T(2,128)(2,1)S(1)}, u32[]{:S(2)}, u32[]{:S(2)}) async-start(bf16[16,2,384]{2,1,0:T(2,128)(2,1)} %reshape.349), calls=%async_computation.7 | async-start | bytes 49152 | tf_op jit(solution)/shard_map/all_to_all | solution.py:230
  332.4 11.1 %all-to-all-start.9 = ((bf16[16,192,32]{1,2,0:T(8,128)(2,1)}), bf16[16,192,32]{1,2,0:T(8,128)(2,1)S(1)}, u32[]{:S(2)}, u32[]{:S(2)}) async-start(bf16[16,192,32]{1,2,0:T(8,128)(2,1)} %copy.160), calls=%async_computation.9 | async-start | bytes 524288 | tf_op jit(solution)/shard_map/all_to_all | solution.py:233
  (10 other events, 104.7 us)
Sparse Core Ops, SparseCore 0:
  11.0 64.0 all-gather.6
  126.8 74.4 all-gather.8
  211.7 50.4 all-gather.12
  264.5 37.7 all-gather.10
where the time goes:
time: 356 us; the launch traced here: 353 us
  waiting for transfers between devices  89 us (25%)
  starting transfers between devices  72.2 us (20%)
  blocking collectives  69.2 us (19%)
  local copies, waits for them, and re-layouts  43.4 us (12%)
  other arithmetic  33.2 us (9%)
  matrix products  31.8 us (9%)
  between operations  14.5 us (4%)
    all_gather x2, blocking collectives, over_pieces(): return lax.all_gather(array, axis).astype(jnp.float32).sum(0)  51.8 us
    all_to_all x2, waiting for transfers between devices, copy_for_each(): lax.all_to_all(jnp.broadcast_to(array[None], (length, *array.shape)), axi...  23.7 us
    all_gather x1, blocking collectives, side_by_side(): lax.all_gather(both, axis, axis=dim, tiled=True)  17.4 us
    scatter-add x1, other arithmetic, shards(): jax.ops.segment_sum(sender_grad, sender_slot, num_segments=lookup_table.s...  17.4 us
    dot_general x8, matrix products, matmul_back(): lax.dot_general(first_operand, second_operand, (((1,), (1,)), ((), ())),...  11.9 us
    gather x1, local copies, waits for them, and re-layouts, shards(): senders = lookup_table[sender_slot]  11.5 us
    all_to_all x1, starting transfers between devices, shards(): lax.all_to_all(outgoing, 'region', split_axis=0, concat_axis=0, tiled=True)  10.6 us
    all_to_all x1, waiting for transfers between devices, shards(): lax.all_to_all(hidden_rows, 'feat', split_axis=1, concat_axis=0, tiled=True)  9.9 us
  transfers between devices with their start and end apart: 18, of which 12 were waited for; matrix products, arithmetic and copies ran while one was open for 24% of the time, Pallas kernels for 0%

commit v1 on v0

v1 whole, which is shorter than its diff:
```python
import jax
import jax.numpy as jnp
from jax import lax
from jax.experimental import pallas as pl
from jax.experimental.pallas import tpu as pltpu
from jax.sharding import PartitionSpec as P

MESH = pl.DeviceIdType.MESH
BF16, F32 = jnp.bfloat16, jnp.float32
EPSILON = 1e-05
SIDE = 4
EDGE_W, NODE_W = (0, 4), (4, 3)


def dot(a, b, da, db):
    return lax.dot_general(a, b, (((da,), (db,)), ((), ())), preferred_element_type=F32)


def mm(a, b):
    return dot(a, b, 1, 0)


def mm_back(a, b):
    return dot(a, b, 1, 1)


def mm_t(a, b):
    return dot(a, b, 0, 0)


def sigmoid(v):
    return 1.0 / (1.0 + jnp.exp(-v))


def layer_norm(m):
    width = m.shape[1]
    mean = jnp.sum(m, axis=1, keepdims=True) / width
    var = jnp.sum(m * m, axis=1, keepdims=True) / width - mean * mean
    inverse = lax.rsqrt(var + EPSILON)
    return (m - mean) * inverse, inverse


def layer_norm_back(cot, normed, inverse, gain):
    width = cot.shape[1]
    s = cot * gain
    first = jnp.sum(s, axis=1, keepdims=True) / width
    second = jnp.sum(s * normed, axis=1, keepdims=True) / width
    return (inverse * (s - first - normed * second)).astype(BF16)


def rows_equal(count, index, base=0):
    rows = lax.broadcasted_iota(jnp.int32, (count, index.shape[1]), 0) + base
    return jnp.where(rows == index, 1.0, 0.0).astype(BF16)


def kernel(regions, feats, scales,
           node, edge, recv_at, send_at, listed, wei, weo, wni, wno, egain, ngain, ncot, ecot,
           node_new, edge_new, node_grad, edge_grad, wgrad,
           nodes, gains, w, outgo, income, pre, normed, srows, rrows, hid, emg,
           pool_s, pool_r, npg, ng_s, ng_r, rem_s, rem_r, ret_s, ret_r, dist_s, dist_r,
           dw, pe_s, pe_r, pn_s, pn_r, re_s, re_r, rn_s, rn_r, qe_s, qe_r, qn_s, qn_r,
           ze_s, ze_r, zn_s, zn_r, be_s, be_r, bn_s, bn_r, ssem, rsem):
    g, f = lax.axis_index("region"), lax.axis_index("feat")
    c, z = lax.rem(g, 2), lax.div(g, 2)
    y, x = lax.div(f, SIDE), lax.rem(f, SIDE)
    sibling = g + 1 - 2 * c
    first = c == 0
    a = jnp.where(first, x, y)
    b = jnp.where(first, y, x)
    chips = regions // 2
    per = node.shape[0]
    width = node.shape[1]
    count = per * feats
    far = income.shape[0] * income.shape[1]

    def feat_at(a_, b_):
        return jnp.where(first, SIDE * b_ + a_, SIDE * a_ + b_)

    def send(src, dst, k, region, feat):
        return pltpu.make_async_remote_copy(
            src_ref=src, dst_ref=dst, send_sem=ssem.at[k], recv_sem=rsem.at[k],
            device_id=(region, feat), device_id_type=MESH)

    def to_plane(src_of, dst, k):
        def body(j, carry):
            t = lax.rem(f + j, feats)
            send(src_of(t), dst.at[f], k, g, t).start()
            return carry
        lax.fori_loop(1, feats, body, 0)

    def to_line(src_of, dst, k):
        def body(j, carry):
            t = lax.rem(g + j, regions)
            send(src_of(t), dst.at[g], k, t, f).start()
            return carry
        lax.fori_loop(1, regions, body, 0)

    def settle(view, k):
        send(view, view, k, g, f).wait()

    barrier = pltpu.get_barrier_semaphore()

    def greet(j, carry):
        pl.semaphore_signal(barrier, inc=1, device_id=(g, lax.rem(f + j, feats)), device_id_type=MESH)
        pl.semaphore_signal(barrier, inc=1, device_id=(lax.rem(g + j, regions), f), device_id_type=MESH)
        return carry
    lax.fori_loop(1, feats, greet, 0)

    lanes = lax.broadcasted_iota(jnp.int32, (egain.shape[1], width), 1)
    lines = lax.broadcasted_iota(jnp.int32, (egain.shape[1], width), 0)
    place = jnp.where(lanes == lines + f * egain.shape[1], 1.0, 0.0)
    both = jnp.concatenate([egain[...], ngain[...]], axis=0)
    gains[f] = lax.dot_general(both, place, (((1,), (0,)), ((), ())), precision=lax.Precision.HIGHEST,
                               preferred_element_type=F32)
    nodes[f] = node[...]
    for k in range(3):
        w[k, y, x, c] = wei[k, c]
    w[3, y, x, c] = weo[c]
    for k in range(2):
        w[4 + k, y, x, c] = wni[k, c]
    w[6, y, x, c] = wno[c]
    income[g] = jnp.zeros(income.shape[1:], BF16)
    ret_r[g] = jnp.zeros(ret_r.shape[1:], BF16)
    pl.semaphore_wait(barrier, feats - 1 + regions - 1)

    to_plane(lambda t: node, nodes, 0)
    to_plane(lambda t: gains.at[f], gains, 1)

    def weights_first(group, k):
        ks = pl.ds(*group)
        for d in range(1, SIDE):
            t = feat_at(lax.rem(a + d, SIDE), b)
            send(w.at[ks, y, x, c], w.at[ks, y, x, c], k, g, t).start()

    def weights_second(group, k, k2):
        ks = pl.ds(*group)
        settle(w.at[ks, 0, pl.ds(0, SIDE - 1), 0], k)

        @pl.when(first)
        def _():
            for d in range(1, SIDE):
                part = w.at[ks, y, :, 0]
                send(part, part, k2, g, SIDE * lax.rem(y + d, SIDE) + x).start()

        @pl.when(c == 1)
        def _():
            for d in range(1, SIDE):
                part = w.at[ks, :, x, 1]
                send(part, part, k2, g, SIDE * y + lax.rem(x + d, SIDE)).start()

    def weights_pass(group, k2, k3):
        ks = pl.ds(*group)
        settle(w.at[ks, pl.ds(0, SIDE - 1), :, 0], k2)
        send(w.at[ks, :, :, c], w.at[ks, :, :, c], k3, sibling, f).start()

    def weights_end(group, k3):
        settle(w.at[pl.ds(*group), :, :, 0], k3)

    weights_first(EDGE_W, 2)
    settle(nodes.at[pl.ds(0, feats - 1)], 0)
    table = nodes[...].reshape(count, width)
    picked = mm_t(rows_equal(count, listed[...]), table).astype(BF16)
    outgo[...] = picked.reshape(outgo.shape)
    to_line(lambda t: outgo.at[t], income, 3)
    weights_second(EDGE_W, 2, 4)
    weights_first(NODE_W, 5)

    into = rows_equal(count, recv_at[...])
    near = rows_equal(count, send_at[...])
    rrows[...] = mm_t(into, table).astype(BF16)
    near_rows = mm_t(near, table)

    weights_pass(EDGE_W, 4, 6)
    weights_second(NODE_W, 5, 7)
    settle(income.at[pl.ds(0, regions - 1)], 3)
    away = rows_equal(far, send_at[...], count)
    srows[...] = (near_rows + mm_t(away, income[...].reshape(far, width))).astype(BF16)
    settle(gains.at[pl.ds(0, feats - 1)], 1)
    gain = jnp.sum(gains[...], axis=0)
    weights_end(EDGE_W, 6)

    def weight(k):
        return w[k].reshape(width, width)

    pre[...] = mm(edge[...], weight(0)) + mm(srows[...], weight(1)) + mm(rrows[...], weight(2))
    hid[...] = (pre[...] * sigmoid(pre[...])).astype(BF16)
    edge_normed, edge_inverse = layer_norm(mm(hid[...], weight(3)))
    normed[...] = edge_normed
    fresh = (edge[...].astype(F32) + edge_normed * gain[0:1]).astype(BF16)
    edge_new[...] = fresh
    pool_s[...] = mm(into, fresh).astype(BF16).reshape(pool_s.shape)
    pool_r[f] = pool_s[f]
    to_plane(lambda t: pool_s.at[t], pool_r, 8)
    weights_pass(NODE_W, 7, 9)
    weights_end(NODE_W, 9)
    settle(pool_r.at[pl.ds(0, feats - 1)], 8)

    pooled = jnp.sum(pool_r[...].astype(F32), axis=0).astype(BF16)
    lat = node[...]
    node_pre = mm(lat, weight(4)) + mm(pooled, weight(5))
    gate = sigmoid(node_pre)
    node_hid = (node_pre * gate).astype(BF16)
    node_normed, node_inverse = layer_norm(mm(node_hid, weight(6)))
    node_new[...] = (lat.astype(F32) + node_normed * gain[1:2]).astype(BF16)
    nmg = layer_norm_back(ncot[...].astype(F32), node_normed, node_inverse, gain[1:2])
    slope = gate * (1.0 + node_pre * (1.0 - gate))
    own_npg = (mm_back(nmg, weight(6)) * slope).astype(BF16)
    npg[f] = own_npg
    to_plane(lambda t: npg.at[f], npg, 10)

    def trade(group, products, out, back, k):
        start, n = group
        for i in range(n):
            dw[start + i] = products(i).reshape(dw.shape[1:])
            out[i] = dw[start + i, :, 1 - c].astype(BF16)
        send(out, back, k, sibling, f).start()

    def along_a(group, out, back, stage, landed, k, k2):
        start, n = group
        settle(back, k)

        def body(j, carry):
            a_, b_ = lax.div(j, SIDE), lax.rem(j, SIDE)
            at = feat_at(a_, b_)
            for i in range(n):
                stage[a_, i, b_] = (dw[start + i, at, c] + back[i, at].astype(F32)).astype(BF16)
            return carry
        lax.fori_loop(0, feats, body, 0)
        landed[a] = stage[a]
        for d in range(1, SIDE):
            a_ = lax.rem(a + d, SIDE)
            send(stage.at[a_], landed.at[a], k2, g, feat_at(a_, b)).start()

    def along_b(landed, stage, landed2, k2, k3):
        settle(landed.at[pl.ds(0, SIDE - 1)], k2)

        def body(b_, carry):
            stage[b_] = jnp.sum(landed[:, :, b_].astype(F32), axis=0).astype(BF16)
            return carry
        lax.fori_loop(0, SIDE, body, 0)
        landed2[b] = stage[b]
        for d in range(1, SIDE):
            b_ = lax.rem(b + d, SIDE)
            send(stage.at[b_], landed2.at[b], k3, g, feat_at(a, b_)).start()

    def along_z(landed, stage, landed2, k3, k4):
        settle(landed.at[pl.ds(0, SIDE - 1)], k3)
        stage[...] = jnp.sum(landed[...].astype(F32), axis=0).astype(BF16)
        landed2[z] = stage[...]
        for d in range(1, chips):
            send(stage, landed2.at[z], k4, lax.rem(g + 2 * d, regions), f).start()

    def to_sibling(group, landed, stage, landed2, k4, k5, scale):
        settle(landed.at[pl.ds(0, chips - 1)], k4)
        stage[...] = jnp.sum(landed[...].astype(F32), axis=0) * scale
        send(stage, landed2, k5, sibling, f).start()
        wgrad[pl.ds(*group), c] = stage[...]

    def finish(group, landed, k5):
        settle(landed, k5)
        wgrad[pl.ds(*group), 1 - c] = landed[...]

    node_sides = ((lat, own_npg), (pooled, own_npg), (node_hid, nmg))
    trade(NODE_W, lambda i: mm_t(*node_sides[i]), pn_s, pn_r, 11)
    direct = ncot[...].astype(F32) + mm_back(own_npg, weight(4))
    along_a(NODE_W, pn_s, pn_r, rn_s, rn_r, 11, 12)
    settle(npg.at[pl.ds(0, feats - 1)], 10)

    reached = mm_t(into, npg[...].reshape(count, width)).astype(BF16)
    total = ecot[...].astype(F32) + mm_back(reached, weight(5))
    emg[...] = layer_norm_back(total, normed[...], edge_inverse, gain[0:1])
    gate = sigmoid(pre[...])
    slope = gate * (1.0 + pre[...] * (1.0 - gate))
    pre_grad = (mm_back(emg[...], weight(3)) * slope).astype(BF16)
    from_send = mm_back(pre_grad, weight(1)).astype(BF16)
    from_recv = mm_back(pre_grad, weight(2)).astype(BF16)
    rem_s[...] = mm(away, from_send).astype(BF16).reshape(rem_s.shape)
    rem_r[f] = rem_s[f]
    to_plane(lambda t: rem_s.at[t], rem_r, 13)
    ng_s[...] = (mm(near, from_send) + mm(into, from_recv)).astype(BF16).reshape(ng_s.shape)
    ng_r[f] = ng_s[f]
    to_plane(lambda t: ng_s.at[t], ng_r, 14)
    edge_grad[...] = total + mm_back(pre_grad, weight(0))
    edge_sides = ((edge, None), (srows, None), (rrows, None), (hid, emg))
    trade(EDGE_W, lambda i: mm_t(edge_sides[i][0][...], pre_grad if i < 3 else emg[...]), pe_s, pe_r, 15)
    along_b(rn_r, qn_s, qn_r, 12, 16)
    along_a(EDGE_W, pe_s, pe_r, re_s, re_r, 15, 17)

    settle(rem_r.at[pl.ds(0, feats - 1)], 13)
    ret_s[...] = jnp.sum(rem_r[...].astype(F32), axis=0).astype(BF16)

    @pl.when(g != f)
    def _():
        send(ret_s, ret_r.at[g], 18, f, f).start()

    along_z(qn_r, zn_s, zn_r, 16, 19)
    along_b(re_r, qe_s, qe_r, 17, 20)

    @pl.when(g == f)
    def _():
        send(ret_r.at[pl.ds(0, regions - 1)], ret_r.at[pl.ds(0, regions - 1)], 18, g, f).wait_recv()
        back = mm(rows_equal(count, listed[...]), ret_r[...].reshape(far, width))
        dist_s[...] = back.astype(BF16).reshape(dist_s.shape)
        dist_r[...] = dist_s[f]
        for d in range(1, feats):
            t = lax.rem(f + d, feats)
            send(dist_s.at[t], dist_r, 21, g, t).start()

    along_z(qe_r, ze_s, ze_r, 20, 22)
    settle(ng_r.at[pl.ds(0, feats - 1)], 14)

    @pl.when(g != f)
    def _():
        send(ret_s, ret_s, 18, f, f).wait_send()
        send(dist_r, dist_r, 21, g, f).wait_recv()

    node_grad[...] = direct + jnp.sum(ng_r[...].astype(F32), axis=0) + dist_r[...].astype(F32)
    to_sibling(NODE_W, zn_r, bn_s, bn_r, 19, 23, scales[1])
    to_sibling(EDGE_W, ze_r, be_s, be_r, 22, 24, scales[0])
    finish(NODE_W, bn_r, 23)
    finish(EDGE_W, be_r, 24)

    @pl.when(g == f)
    def _():
        send(dist_s.at[pl.ds(0, feats - 1)], dist_s.at[pl.ds(0, feats - 1)], 21, g, f).wait_send()


def shards(sizes, node_lat, edge_lat, receiver_row, sender_slot, send_rows, w_edge_in, w_edge_out, w_node_in,
           w_node_out, edge_gain, node_gain, node_cot, edge_cot):
    regions, feats = sizes
    per, width = node_lat.shape
    edges = edge_lat.shape[0]
    slots = send_rows.shape[2]
    part = width // feats // 2
    f = lax.axis_index("feat")
    recv_at = lax.dynamic_slice_in_dim(receiver_row, f * edges, edges)[None]
    send_at = lax.dynamic_slice_in_dim(sender_slot, f * edges, edges)[None]
    listed = send_rows.reshape(1, regions * slots)
    scales = (1.0 / float(edges * feats * regions) ** 0.5, 1.0 / float(per * feats * regions) ** 0.5)
    ne, nn = EDGE_W[1], NODE_W[1]

    def v(dtype, *shape):
        return pltpu.VMEM(shape, dtype)

    nodes_like = (feats, per, width)
    line_like = (regions, slots, width)

    def pair(dtype, *shape):
        return [v(dtype, *shape)] * 2

    scratch = [
        v(BF16, *nodes_like), v(F32, feats, 2, width), v(BF16, ne + nn, SIDE, SIDE, 2, part, width),
        *pair(BF16, *line_like),
        *pair(F32, edges, width),
        *[v(BF16, edges, width)] * 4,
        *pair(BF16, *nodes_like), v(BF16, *nodes_like), *pair(BF16, *nodes_like), *pair(BF16, *line_like),
        v(BF16, slots, width), v(BF16, *line_like), v(BF16, *nodes_like), v(BF16, per, width),
        v(F32, ne + nn, feats, 2, part, width),
        *pair(BF16, ne, feats, part, width), *pair(BF16, nn, feats, part, width),
        *pair(BF16, SIDE, ne, SIDE, part, width), *pair(BF16, SIDE, nn, SIDE, part, width),
        *pair(BF16, SIDE, ne, part, width), *pair(BF16, SIDE, nn, part, width),
        v(BF16, ne, part, width), v(BF16, regions // 2, ne, part, width),
        v(BF16, nn, part, width), v(BF16, regions // 2, nn, part, width),
        *pair(F32, ne, part, width), *pair(F32, nn, part, width),
        pltpu.SemaphoreType.DMA((25,)), pltpu.SemaphoreType.DMA((25,)),
    ]

    def body(*refs):
        kernel(regions, feats, scales, *refs)

    vmem = pl.BlockSpec(memory_space=pltpu.VMEM)
    node_new, edge_new, node_grad, edge_grad, wgrad = pl.pallas_call(
        body,
        name="layer",
        out_shape=(
            jax.ShapeDtypeStruct((per, width), BF16), jax.ShapeDtypeStruct((edges, width), BF16),
            jax.ShapeDtypeStruct((per, width), F32), jax.ShapeDtypeStruct((edges, width), F32),
            jax.ShapeDtypeStruct((ne + nn, 2, part, width), F32),
        ),
        in_specs=[vmem] * 13,
        out_specs=[vmem] * 5,
        scratch_shapes=scratch,
        compiler_params=pltpu.CompilerParams(
            collective_id=0, has_side_effects=True, vmem_limit_bytes=60 * 2**20),
    )(node_lat, edge_lat, recv_at, send_at, listed,
      w_edge_in.reshape(3, 2, part, width), w_edge_out.reshape(2, part, width),
      w_node_in.reshape(2, 2, part, width), w_node_out.reshape(2, part, width),
      edge_gain[None], node_gain[None], node_cot, edge_cot)
    wgrad = wgrad.reshape(ne + nn, 2 * part, width)
    return node_new, edge_new, node_grad, edge_grad, wgrad[:3], wgrad[3], wgrad[4:6], wgrad[6]


def solution(mesh):
    rows = P(("region", "feat"), None)
    blocks = (P(None, "feat", None), P("feat", None), P(None, "feat", None), P("feat", None))
    in_specs = (rows, rows, P("region"), P("region"), P("region", None, None), *blocks, P("feat"), P("feat"), rows, rows)
    sizes = (mesh.shape["region"], mesh.shape["feat"])
    return jax.shard_map(lambda *args: shards(sizes, *args), mesh=mesh, in_specs=in_specs,
                         out_specs=(rows, rows, rows, rows, *blocks), check_vma=False)
```

time: 356 us -> 103 us (0.29)
  Pallas kernels: 0 us -> 90.9 us
  waiting for transfers between devices: 89 us -> 0 us
  starting transfers between devices: 72.2 us -> 0 us
  blocking collectives: 69.2 us -> 0 us
  other arithmetic: 33.2 us -> 0 us
  local copies, waits for them, and re-layouts: 43.4 us -> 10.9 us
  matrix products: 31.8 us -> 0 us
  between operations: 14.5 us -> 0.66 us
    pallas_call x0 -> x1, Pallas kernels: none -> 90.9 us  [shards(): pl.pallas_call(body, name='layer', out_shape=(jax.ShapeDtypeStruct((per,...]
    all_to_all x14 -> x0, waiting for transfers between devices: 81.8 us -> none  [the longest x2 23.7 us: copy_for_each(): lax.all_to_all(jnp.broadcast_to(array[None], (length, *array.shape)), axi...]
    all_to_all x14 -> x0, starting transfers between devices: 72 us -> none  [the longest x1 10.6 us: shards(): lax.all_to_all(outgoing, 'region', split_axis=0, concat_axis=0, tiled=True)]
    all_gather x3 -> x0, blocking collectives: 69.2 us -> none  [the longest x2 51.8 us: over_pieces(): return lax.all_gather(array, axis).astype(jnp.float32).sum(0)]
    dot_general x25 -> x0, matrix products: 31.8 us -> none  [the longest x8 11.9 us: matmul_back(): lax.dot_general(first_operand, second_operand, (((1,), (1,)), ((), ())),...]
    gather x7 -> x0, local copies, waits for them, and re-layouts: 24.6 us -> none  [the longest x1 11.5 us: shards(): senders = lookup_table[sender_slot]]
    scatter-add x2 -> x0, other arithmetic: 19.5 us -> none  [the longest x1 17.4 us: shards(): jax.ops.segment_sum(sender_grad, sender_slot, num_segments=lookup_table.s...]
    all_gather x4 -> x0, waiting for transfers between devices: 7.08 us -> none  [the longest x2 7.06 us: over_pieces(): return lax.all_gather(array, axis).astype(jnp.float32).sum(0)]
  transfers between devices with their start and end apart: 18 -> 0, of which waited for: 12 -> 0; matrix products, arithmetic and copies ran while one was open for 24% -> 0% of each run, Pallas kernels for 0% -> 0%
where the time goes in v1:
time: 103 us; the launch traced here: 102 us
  Pallas kernels  90.9 us (88%)
  local copies, waits for them, and re-layouts  10.9 us (11%)
    pallas_call x1, Pallas kernels, shards(): pl.pallas_call(body, name='layer', out_shape=(jax.ShapeDtypeStruct((per,...  90.9 us
    unnamed x14, local copies, waits for them, and re-layouts  2.79 us

profile of v1, /device:TPU:1, one launch (start us, length us, event | category | flops | bytes accessed | tf_op | source)
XLA Modules:
  0.0 102.5 jit_solution(16264656125283024203)
XLA Ops:
  0.6 0.0 copy-start.4
  0.6 1.3 %dynamic_slice.6 = s32[192]{0:T(256)} dynamic-slice(s32[3072]{0:T(1024)} %param.15, s32[]{:T(128)S(6)} %select_n.4), dynamic_slice_sizes={192} | dynamic-slice | bytes 1540 | tf_op jit(solution)/shard_map/dynamic_slice | solution.py:336
  2.0 1.3 %dynamic_slice.7 = s32[192]{0:T(256)} dynamic-slice(s32[3072]{0:T(1024)} %param.16, s32[]{:T(128)S(6)} %select_n.4), dynamic_slice_sizes={192} | dynamic-slice | bytes 1540 | tf_op jit(solution)/shard_map/dynamic_slice | solution.py:337
  3.3 0.0 copy-done.4
  3.3 0.6 reshape.38.refs_4_
  4.0 90.9 %layer.1 = (bf16[24,512]{1,0:T(8,128)(2,1)}, bf16[192,512]{1,0:T(8,128)(2,1)}, f32[24,512]{1,0:T(8,128)}, f32[192,512]{1,0:T(8,128)}, f32[7,2,16,512]{3,2,1,0:T(8,128)}) custom-call(bf16[24,512]{1,0:T(8,128)(2,1)} %refs_0_.1, bf16[192,512]{1,0:T(8,128)(2,1)} %refs_1_.1, s32[1,192]{1,0:T(1,128)} %bitcast.20, s32[1,192]{1,0:T(1,128)} %bitcast.21, ...), custom_call_target="tpu_custom_call" | custom-call | tf_op jit(solution)/shard_map/layer/pallas_call | solution.py:372
  94.9 1.6 %slice.23 = f32[2,2,16,512]{3,2,1,0:T(8,128)} slice(f32[7,2,16,512]{3,2,1,0:T(8,128)} %get-tuple-element.17), slice={[4:6], [0:2], [0:16], [0:512]} | slice | bytes 262144 | tf_op jit(solution)/shard_map/slice | solution.py:390
  96.5 0.0 copy-start.3
  96.5 0.0 copy-start.1
  96.5 1.6 %fusion = (f32[1,2,16,512]{3,2,1,0:T(8,128)}, f32[1,2,16,512]{3,2,1,0:T(8,128)}) fusion(f32[7,2,16,512]{3,2,1,0:T(8,128)} %get-tuple-element.17), kind=kLoop, calls=%fused_computation | loop fusion | bytes 262144 | tf_op jit(solution)/shard_map/slice | solution.py:390
  98.0 0.0 copy-start
  98.0 1.7 %slice.20 = f32[3,2,16,512]{3,2,1,0:T(8,128)} slice(f32[7,2,16,512]{3,2,1,0:T(8,128)} %get-tuple-element.17), slice={[0:3], [0:2], [0:16], [0:512]} | slice | bytes 393216 | tf_op jit(solution)/shard_map/slice | solution.py:390
  99.7 0.0 copy-done.3
  99.7 0.6 copy.25
  100.3 0.0 copy-done.1
  100.3 0.0 copy-start.2
  100.3 0.7 copy.26
  101.0 0.1 copy-done.2
  101.1 0.6 copy.27
  101.7 0.0 copy-done
  101.7 0.7 copy.28
Async XLA Ops:
  0.6 2.7 %copy-start.4 = (s32[1,16,16]{2,1,0:T(8,128)S(1)}, s32[1,16,16]{2,1,0:T(8,128)}, u32[]{:S(2)}) copy-start(s32[1,16,16]{2,1,0:T(8,128)} %param.17) | copy-start | bytes 3076
  96.5 3.2 %copy-start.3 = (bf16[24,512]{1,0:T(8,128)(2,1)S(1)}, bf16[24,512]{1,0:T(8,128)(2,1)}, u32[]{:S(2)}) copy-start(bf16[24,512]{1,0:T(8,128)(2,1)} %get-tuple-element.28) | copy-start | bytes 73732
  96.5 3.9 %copy-start.1 = (bf16[192,512]{1,0:T(8,128)(2,1)S(1)}, bf16[192,512]{1,0:T(8,128)(2,1)}, u32[]{:S(2)}) copy-start(bf16[192,512]{1,0:T(8,128)(2,1)} %get-tuple-element.29) | copy-start | bytes 589828
  98.0 3.7 %copy-start = (f32[192,512]{1,0:T(8,128)S(1)}, f32[192,512]{1,0:T(8,128)}, u32[]{:S(2)}) copy-start(f32[192,512]{1,0:T(8,128)} %get-tuple-element.31) | copy-start | bytes 1179652
  100.3 0.8 copy-start.2

commit v2 on v1

v2 whole, which is shorter than its diff:
```python
import jax
import jax.numpy as jnp
from jax import lax
from jax.experimental import pallas as pl
from jax.experimental.pallas import tpu as pltpu
from jax.sharding import PartitionSpec as P

MESH = pl.DeviceIdType.MESH
BF16, F32 = jnp.bfloat16, jnp.float32
EPSILON = 1e-05
SIDE = 4
EDGE_W, NODE_W = (0, 4), (4, 3)
VMEM_LIMIT = 44 * 2**20


def dot(a, b, da, db):
    return lax.dot_general(a, b, (((da,), (db,)), ((), ())), preferred_element_type=F32)


def mm(a, b):
    return dot(a, b, 1, 0)


def mm_back(a, b):
    return dot(a, b, 1, 1)


def mm_t(a, b):
    return dot(a, b, 0, 0)


def sigmoid(v):
    return 1.0 / (1.0 + jnp.exp(-v))


def layer_norm(m):
    width = m.shape[1]
    mean = jnp.sum(m, axis=1, keepdims=True) / width
    var = jnp.sum(m * m, axis=1, keepdims=True) / width - mean * mean
    inverse = lax.rsqrt(var + EPSILON)
    return (m - mean) * inverse, inverse


def layer_norm_back(cot, normed, inverse, gain):
    width = cot.shape[1]
    s = cot * gain
    first = jnp.sum(s, axis=1, keepdims=True) / width
    second = jnp.sum(s * normed, axis=1, keepdims=True) / width
    return (inverse * (s - first - normed * second)).astype(BF16)


def iota(shape, dim):
    return lax.broadcasted_iota(jnp.int32, shape, dim)


def rows_equal(count, index, base=0):
    rows = iota((count, index.shape[1]), 0) + base
    return jnp.where(rows == index, 1.0, 0.0).astype(BF16)


def flat(blocks, pick, mine):
    wide = lax.dot_general(blocks, jnp.where(pick, 1.0, 0.0), (((1,), (0,)), ((), ())),
                           precision=lax.Precision.HIGHEST, preferred_element_type=F32)
    return jnp.sum(jnp.where(mine, wide, 0.0), axis=0, keepdims=True)


def own_slice(ref, f, edges):
    lines = 2 * edges // 128
    start = lax.div(f, 2) * lines
    two = jnp.concatenate([ref[start + i] for i in range(lines)], axis=1)
    return jnp.where(lax.rem(f, 2) == 1, two[:, edges:], two[:, :edges])


def kernel(regions, feats, scales, fetches,
           node, edge, recv_all, send_all, listed_at, wei, weo, wni, wno, egain, ngain, ncot, ecot,
           node_new, edge_new, node_grad, edge_grad, wgrad,
           nodes, gains, w, outgo, income, pre, normed, srows, rrows, hid, emg,
           pool_s, pool_r, npg, ng_s, ng_r, rem_s, rem_r, ret_s, ret_r, dist_s, dist_r,
           dw, pe_s, pe_r, pn_s, pn_r, re_s, re_r, rn_s, rn_r, qe_s, qe_r, qn_s, qn_r,
           ze_s, ze_r, zn_s, zn_r, be, bn, ssem, rsem):
    g, f = lax.axis_index("region"), lax.axis_index("feat")
    c, z = lax.rem(g, 2), lax.div(g, 2)
    y, x = lax.div(f, SIDE), lax.rem(f, SIDE)
    sibling = g + 1 - 2 * c
    first = c == 0
    a = jnp.where(first, x, y)
    b = jnp.where(first, y, x)
    chips = regions // 2
    per, width = node.shape
    edges = edge.shape[0]
    count = per * feats
    slots = income.shape[1]
    far = regions * slots

    def feat_at(a_, b_):
        return jnp.where(first, SIDE * b_ + a_, SIDE * a_ + b_)

    def send(src, dst, k, region, feat):
        return pltpu.make_async_remote_copy(
            src_ref=src, dst_ref=dst, send_sem=ssem.at[k], recv_sem=rsem.at[k],
            device_id=(region, feat), device_id_type=MESH)

    def to_plane(src_of, dst, k):
        def body(j, carry):
            t = lax.rem(f + j, feats)
            send(src_of(t), dst.at[f], k, g, t).start()
            return carry
        lax.fori_loop(1, feats, body, 0)

    def to_line(src_of, dst, k):
        def body(j, carry):
            t = lax.rem(g + j, regions)
            send(src_of(t), dst.at[g], k, t, f).start()
            return carry
        lax.fori_loop(1, regions, body, 0)

    def settle(view, k):
        send(view, view, k, g, f).wait()

    def settle_slots(buffer, k):
        settle(buffer.at[pl.ds(0, buffer.shape[0] - 1)], k)

    barrier = pltpu.get_barrier_semaphore()

    def greet(j, carry):
        pl.semaphore_signal(barrier, inc=1, device_id=(g, lax.rem(f + j, feats)), device_id_type=MESH)
        pl.semaphore_signal(barrier, inc=1, device_id=(lax.rem(g + j, regions), f), device_id_type=MESH)
        return carry
    lax.fori_loop(1, feats, greet, 0)
    for fetch in fetches:
        fetch.wait()

    portion = egain.shape[1]
    gains[f] = jnp.concatenate([egain[...], ngain[...], jnp.zeros((1, gains.shape[2] - 2 * portion), F32)], axis=1)
    nodes[f] = node[...]
    for k in range(3):
        w[k, y, x, c] = wei[k, c]
    w[3, y, x, c] = weo[c]
    for k in range(2):
        w[4 + k, y, x, c] = wni[k, c]
    w[6, y, x, c] = wno[c]
    income[g] = jnp.zeros(income.shape[1:], BF16)
    ret_r[g] = jnp.zeros(ret_r.shape[1:], BF16)
    recv_at = own_slice(recv_all, f, edges)
    send_at = own_slice(send_all, f, edges)
    grid = (regions, far)
    listed = flat(listed_at[0].astype(F32), lax.rem(iota((slots, far), 1), slots) == iota((slots, far), 0),
                  lax.div(iota(grid, 1), slots) == iota(grid, 0))
    asked = jnp.where(iota((count, far), 0).astype(F32) == listed, 1.0, 0.0).astype(BF16)
    into = rows_equal(count, recv_at)
    near = rows_equal(count, send_at)
    away = rows_equal(far, send_at, count)
    pl.semaphore_wait(barrier, feats - 1 + regions - 1)

    def weights_first(group, k):
        part = w.at[pl.ds(*group), y, x, c]
        for d in range(1, SIDE):
            send(part, part, k, g, feat_at(lax.rem(a + d, SIDE), b)).start()

    def bundle(group, b_, act):
        ks = pl.ds(*group)

        @pl.when(first)
        def _():
            act(w.at[ks, b_, :, 0])

        @pl.when(c == 1)
        def _():
            act(w.at[ks, :, b_, 1])

    def weights_second(group, k, k2):
        settle(w.at[pl.ds(*group), 0, pl.ds(0, SIDE - 1), 0], k)

        def act(part):
            for d in range(1, SIDE):
                send(part, part, k2 + d, g, feat_at(a, lax.rem(b + d, SIDE))).start()
            send(part, part, k2, sibling, f).start()
        bundle(group, b, act)

    def weights_pass(group, k2):
        for d in range(1, SIDE):
            settle(w.at[pl.ds(*group), 0, :, 0], k2 + d)
            bundle(group, lax.rem(b - d + SIDE, SIDE), lambda part: send(part, part, k2, sibling, f).start())

    def weights_end(group, k2):
        settle(w.at[pl.ds(*group), :, :, 0], k2)

    to_plane(lambda t: node, nodes, 0)
    weights_first(EDGE_W, 2)
    weights_first(NODE_W, 3)
    to_plane(lambda t: gains.at[f], gains, 1)
    settle_slots(nodes, 0)
    table = nodes[...].reshape(count, width)
    outgo[...] = mm_t(asked, table).astype(BF16).reshape(outgo.shape)
    to_line(lambda t: outgo.at[t], income, 4)
    weights_second(EDGE_W, 2, 5)
    weights_second(NODE_W, 3, 9)
    rrows[...] = mm_t(into, table).astype(BF16)
    near_rows = mm_t(near, table)
    settle_slots(gains, 1)
    packed = gains[...].reshape(feats, gains.shape[2])
    shape, wide = (gains.shape[2], 2 * width), (feats, 2 * width)
    lanes = iota(shape, 1)
    gain = flat(packed, lax.rem(lanes, portion) + portion * lax.div(lanes, width) == iota(shape, 0),
                lax.div(lax.rem(iota(wide, 1), width), portion) == iota(wide, 0))
    edge_gain, node_gain = gain[:, :width], gain[:, width:]
    weights_pass(EDGE_W, 5)
    settle_slots(income, 4)
    srows[...] = (near_rows + mm_t(away, income[...].reshape(far, width))).astype(BF16)
    weights_end(EDGE_W, 5)

    def weight(k):
        return w[k].reshape(width, width)

    pre[...] = mm(edge[...], weight(0)) + mm(srows[...], weight(1)) + mm(rrows[...], weight(2))
    hid[...] = (pre[...] * sigmoid(pre[...])).astype(BF16)
    edge_normed, edge_inverse = layer_norm(mm(hid[...], weight(3)))
    normed[...] = edge_normed
    fresh = (edge[...].astype(F32) + edge_normed * edge_gain).astype(BF16)
    edge_new[...] = fresh
    pool_s[...] = mm(into, fresh).astype(BF16).reshape(pool_s.shape)
    pool_r[f] = pool_s[f]
    to_plane(lambda t: pool_s.at[t], pool_r, 13)
    weights_pass(NODE_W, 9)
    weights_end(NODE_W, 9)
    settle_slots(pool_r, 13)

    pooled = jnp.sum(pool_r[...].astype(F32), axis=0).astype(BF16)
    lat = node[...]
    node_pre = mm(lat, weight(4)) + mm(pooled, weight(5))
    gate = sigmoid(node_pre)
    node_hid = (node_pre * gate).astype(BF16)
    node_normed, node_inverse = layer_norm(mm(node_hid, weight(6)))
    node_new[...] = (lat.astype(F32) + node_normed * node_gain).astype(BF16)
    nmg = layer_norm_back(ncot[...].astype(F32), node_normed, node_inverse, node_gain)
    slope = gate * (1.0 + node_pre * (1.0 - gate))
    own_npg = (mm_back(nmg, weight(6)) * slope).astype(BF16)
    npg[f] = own_npg
    to_plane(lambda t: npg.at[f], npg, 14)

    def trade(group, products, out, back, k):
        start, n = group
        for i in range(n):
            dw[start + i] = products(i).reshape(dw.shape[1:])
            out[i] = dw[start + i, :, 1 - c].astype(BF16)
        send(out, back, k, sibling, f).start()

    def along_a(group, out, back, stage, landed, k, k2):
        start, n = group
        settle(back, k)

        def body(j, carry):
            a_, b_ = lax.div(j, SIDE), lax.rem(j, SIDE)
            at = feat_at(a_, b_)
            for i in range(n):
                stage[a_, i, b_] = (dw[start + i, at, c] + back[i, at].astype(F32)).astype(BF16)
            return carry
        lax.fori_loop(0, feats, body, 0)
        landed[a] = stage[a]
        for d in range(1, SIDE):
            a_ = lax.rem(a + d, SIDE)
            send(stage.at[a_], landed.at[a], k2, g, feat_at(a_, b)).start()

    def along_b(landed, stage, landed2, k2, k3):
        settle_slots(landed, k2)

        def body(b_, carry):
            stage[b_] = jnp.sum(landed[:, :, b_].astype(F32), axis=0).astype(BF16)
            return carry
        lax.fori_loop(0, SIDE, body, 0)
        landed2[b] = stage[b]
        for d in range(1, SIDE):
            b_ = lax.rem(b + d, SIDE)
            send(stage.at[b_], landed2.at[b], k3, g, feat_at(a, b_)).start()

    def along_z(landed, stage, landed2, k3, k4):
        settle_slots(landed, k3)
        whole = jnp.sum(landed[...].astype(F32), axis=0).astype(BF16)
        rows = stage.shape[1]
        pieces = whole.reshape(whole.shape[0] * whole.shape[1] // rows, rows, width)
        stage[pl.ds(0, pieces.shape[0])] = pieces
        if pieces.shape[0] < chips:
            stage[pl.ds(pieces.shape[0], chips - pieces.shape[0])] = jnp.zeros(
                (chips - pieces.shape[0], rows, width), BF16)
        landed2[z] = stage[z]
        for d in range(1, chips):
            z_ = lax.rem(z + d, chips)
            send(stage.at[z_], landed2.at[z], k4, 2 * z_ + c, f).start()

    def to_all(landed, whole, k4, k5, scale):
        settle_slots(landed, k4)
        whole[g] = (jnp.sum(landed[...].astype(F32), axis=0) * scale).astype(BF16)
        to_line(lambda t: whole.at[g], whole, k5)

    def finish(group, whole, k5):
        settle_slots(whole, k5)
        start, n = group
        rows = whole.shape[1]
        halves = wgrad.shape[2] // rows
        for i in range(n):
            for c_ in range(2):
                for h in range(halves):
                    wgrad[start + i, c_, pl.ds(h * rows, rows)] = whole[2 * (halves * i + h) + c_].astype(F32)

    node_sides = ((lat, own_npg), (pooled, own_npg), (node_hid, nmg))
    trade(NODE_W, lambda i: mm_t(*node_sides[i]), pn_s, pn_r, 15)
    direct = ncot[...].astype(F32) + mm_back(own_npg, weight(4))
    along_a(NODE_W, pn_s, pn_r, rn_s, rn_r, 15, 16)
    settle_slots(npg, 14)

    reached = mm_t(into, npg[...].reshape(count, width)).astype(BF16)
    total = ecot[...].astype(F32) + mm_back(reached, weight(5))
    emg[...] = layer_norm_back(total, normed[...], edge_inverse, edge_gain)
    gate = sigmoid(pre[...])
    slope = gate * (1.0 + pre[...] * (1.0 - gate))
    pre_grad = (mm_back(emg[...], weight(3)) * slope).astype(BF16)
    edge_sides = ((edge, None), (srows, None), (rrows, None), (hid, emg))
    trade(EDGE_W, lambda i: mm_t(edge_sides[i][0][...], pre_grad if i < 3 else emg[...]), pe_s, pe_r, 17)
    from_send = mm_back(pre_grad, weight(1)).astype(BF16)
    rem_s[...] = mm(away, from_send).astype(BF16).reshape(rem_s.shape)
    rem_r[f] = rem_s[f]
    to_plane(lambda t: rem_s.at[t], rem_r, 18)
    from_recv = mm_back(pre_grad, weight(2)).astype(BF16)
    ng_s[...] = (mm(near, from_send) + mm(into, from_recv)).astype(BF16).reshape(ng_s.shape)
    ng_r[f] = ng_s[f]
    edge_grad[...] = total + mm_back(pre_grad, weight(0))
    along_a(EDGE_W, pe_s, pe_r, re_s, re_r, 17, 19)
    along_b(rn_r, qn_s, qn_r, 16, 20)
    to_plane(lambda t: ng_s.at[t], ng_r, 21)

    settle_slots(rem_r, 18)
    ret_s[...] = jnp.sum(rem_r[...].astype(F32), axis=0).astype(BF16)

    @pl.when(g != f)
    def _():
        send(ret_s, ret_r.at[g], 22, f, f).start()

    along_z(qn_r, zn_s, zn_r, 20, 23)
    along_b(re_r, qe_s, qe_r, 19, 24)

    @pl.when(g == f)
    def _():
        send(ret_r.at[pl.ds(0, regions - 1)], ret_r.at[pl.ds(0, regions - 1)], 22, g, f).wait_recv()
        dist_s[...] = mm(asked, ret_r[...].reshape(far, width)).astype(BF16).reshape(dist_s.shape)
        dist_r[...] = dist_s[f]
        for d in range(1, feats):
            t = lax.rem(f + d, feats)
            send(dist_s.at[t], dist_r, 25, g, t).start()

    along_z(qe_r, ze_s, ze_r, 24, 26)
    to_all(zn_r, bn, 23, 27, scales[1])
    to_all(ze_r, be, 26, 28, scales[0])
    settle_slots(ng_r, 21)

    @pl.when(g != f)
    def _():
        send(ret_s, ret_s, 22, f, f).wait_send()
        send(dist_r, dist_r, 25, g, f).wait_recv()

    node_grad[...] = direct + jnp.sum(ng_r[...].astype(F32), axis=0) + dist_r[...].astype(F32)
    finish(NODE_W, bn, 27)
    finish(EDGE_W, be, 28)

    @pl.when(g == f)
    def _():
        send(dist_s.at[pl.ds(0, feats - 1)], dist_s.at[pl.ds(0, feats - 1)], 25, g, f).wait_send()


def hand_on(*refs):
    sources, outs, out = refs[:5], refs[5:13], refs[13]
    grads = sources[4]
    views = [*sources[:4], grads.at[pl.ds(0, 3)], grads.at[3], grads.at[pl.ds(4, 2)], grads.at[6]]
    copies = [pltpu.make_async_copy(v, o, out.at[i]) for i, (v, o) in enumerate(zip(views, outs))]
    for copy in copies:
        copy.start()
    for copy in copies:
        copy.wait()


def shards(sizes, node_lat, edge_lat, receiver_row, sender_slot, send_rows, w_edge_in, w_edge_out, w_node_in,
           w_node_out, edge_gain, node_gain, node_cot, edge_cot):
    regions, feats = sizes
    per, width = node_lat.shape
    edges = edge_lat.shape[0]
    slots = send_rows.shape[2]
    part = width // feats // 2
    lines = (edges * feats // 128, 1, 128)
    scales = (1.0 / float(edges * feats * regions) ** 0.5, 1.0 / float(per * feats * regions) ** 0.5)
    ne, nn = EDGE_W[1], NODE_W[1]
    piece = ne * part // (regions // 2)

    def v(dtype, *shape):
        return pltpu.VMEM(shape, dtype)

    nodes_like = (feats, per, width)
    line_like = (regions, slots, width)

    def pair(dtype, *shape):
        return [v(dtype, *shape)] * 2

    scratch = [
        v(BF16, *nodes_like), v(F32, feats, 1, 128), v(BF16, ne + nn, SIDE, SIDE, 2, part, width),
        *pair(BF16, *line_like),
        *pair(F32, edges, width),
        *[v(BF16, edges, width)] * 4,
        *pair(BF16, *nodes_like), v(BF16, *nodes_like), *pair(BF16, *nodes_like), *pair(BF16, *line_like),
        v(BF16, slots, width), v(BF16, *line_like), v(BF16, *nodes_like), v(BF16, per, width),
        v(F32, ne + nn, feats, 2, part, width),
        *pair(BF16, ne, feats, part, width), *pair(BF16, nn, feats, part, width),
        *pair(BF16, SIDE, ne, SIDE, part, width), *pair(BF16, SIDE, nn, SIDE, part, width),
        *pair(BF16, SIDE, ne, part, width), *pair(BF16, SIDE, nn, part, width),
        *pair(BF16, regions // 2, piece, width), *pair(BF16, regions // 2, piece, width),
        *pair(BF16, regions, piece, width),
        pltpu.SemaphoreType.DMA((29,)), pltpu.SemaphoreType.DMA((29,)),
    ]

    args = (node_lat, edge_lat, receiver_row.reshape(lines), sender_slot.reshape(lines), send_rows,
            w_edge_in.reshape(3, 2, part, width), w_edge_out.reshape(2, part, width),
            w_node_in.reshape(2, 2, part, width), w_node_out.reshape(2, part, width),
            edge_gain[None], node_gain[None], node_cot, edge_cot)
    n = len(args)
    scratch += [*[v(x.dtype, *x.shape) for x in args], pltpu.SemaphoreType.DMA((n,))]

    def body(*refs):
        sources, rest = refs[:n], refs[n:]
        held, sem = rest[-n - 1:-1], rest[-1]
        fetches = [pltpu.make_async_copy(s, h, sem.at[i]) for i, (s, h) in enumerate(zip(sources, held))]
        for fetch in fetches:
            fetch.start()
        kernel(regions, feats, scales, fetches, *held, *rest[:-n - 1])

    vmem = pl.BlockSpec(memory_space=pltpu.VMEM)
    kinds = [((per, width), BF16), ((edges, width), BF16), ((per, width), F32), ((edges, width), F32)]
    blocks = [(3, 2, part, width), (2, part, width), (2, 2, part, width), (2, part, width)]
    results = pl.pallas_call(
        body,
        name="layer",
        out_shape=[jax.ShapeDtypeStruct(*k) for k in (*kinds, ((ne + nn, 2, part, width), F32))],
        in_specs=[pl.BlockSpec(memory_space=pltpu.HBM)] * n,
        out_specs=[vmem] * 5,
        scratch_shapes=scratch,
        compiler_params=pltpu.CompilerParams(
            collective_id=0, has_side_effects=True, vmem_limit_bytes=VMEM_LIMIT),
    )(*[pltpu.with_memory_space_constraint(x, pltpu.HBM) for x in args])
    kinds += [(s, F32) for s in blocks]
    outs = pl.pallas_call(
        hand_on,
        name="hand_on",
        out_shape=[jax.ShapeDtypeStruct(*k) for k in kinds],
        in_specs=[vmem] * 5,
        out_specs=[pl.BlockSpec(memory_space=pltpu.HBM)] * 8,
        scratch_shapes=[pltpu.SemaphoreType.DMA((8,))],
        compiler_params=pltpu.CompilerParams(vmem_limit_bytes=8 * 2**20),
    )(*results)
    return (*outs[:4], outs[4].reshape(3, 2 * part, width), outs[5].reshape(2 * part, width),
            outs[6].reshape(2, 2 * part, width), outs[7].reshape(2 * part, width))


def solution(mesh):
    rows = P(("region", "feat"), None)
    blocks = (P(None, "feat", None), P("feat", None), P(None, "feat", None), P("feat", None))
    in_specs = (rows, rows, P("region"), P("region"), P("region", None, None), *blocks, P("feat"), P("feat"), rows, rows)
    sizes = (mesh.shape["region"], mesh.shape["feat"])
    return jax.shard_map(lambda *args: shards(sizes, *args), mesh=mesh, in_specs=in_specs,
                         out_specs=(rows, rows, rows, rows, *blocks), check_vma=False)
```

time: 103 us -> 82.9 us (0.80)
  local copies, waits for them, and re-layouts: 10.9 us -> 0 us
  Pallas kernels: 90.9 us -> 82.1 us
    pallas_call x1 -> x2, Pallas kernels: 90.9 us -> 82.1 us  [the longest x1 81.1 us: shards(): pl.pallas_call(body, name='layer', out_shape=[jax.ShapeDtypeStruct(*k) fo...]
    slice x3 -> x0, local copies, waits for them, and re-layouts: 4.8 us -> none  [the longest x1 1.67 us: shards(): wgrad[:3]]
    unnamed x14 -> x0, local copies, waits for them, and re-layouts: 2.79 us -> none
    dynamic_slice x2 -> x0, local copies, waits for them, and re-layouts: 2.67 us -> none  [the longest x1 1.34 us: shards(): recv_at = lax.dynamic_slice_in_dim(receiver_row, f * edges, edges)[None]]
where the time goes in v2:
time: 82.9 us; the launch traced here: 82.7 us
  Pallas kernels  82.1 us (99%)
    pallas_call x1, Pallas kernels, shards(): pl.pallas_call(body, name='layer', out_shape=[jax.ShapeDtypeStruct(*k) fo...  81.1 us

profile of v2, /device:TPU:1, one launch (start us, length us, event | category | flops | bytes accessed | tf_op | source)
XLA Modules:
  0.0 82.7 jit_solution(14267129929482175174)
XLA Ops:
  0.6 81.1 %layer.1 = (bf16[24,512]{1,0:T(8,128)(2,1)S(1)}, bf16[192,512]{1,0:T(8,128)(2,1)S(1)}, f32[24,512]{1,0:T(8,128)S(1)}, f32[192,512]{1,0:T(8,128)S(1)}, f32[7,2,16,512]{3,2,1,0:T(8,128)S(1)}) custom-call(bf16[24,512]{1,0:T(8,128)(2,1)} %refs_0_.1, bf16[192,512]{1,0:T(8,128)(2,1)} %refs_1_.1, s32[24,1,128]{2,1,0:T(1,128)} %bitcast.16, s32[24,1,128]{2,1,0:T(1,128)} %bitcast.17, ...), custom_call_target="tpu_custom_call" | custom-call | tf_op jit(solution)/shard_map/layer/pallas_call | solution.py:435
  81.7 1.1 %hand_on.1 = (bf16[24,512]{1,0:T(8,128)(2,1)}, bf16[192,512]{1,0:T(8,128)(2,1)}, f32[24,512]{1,0:T(8,128)}, f32[192,512]{1,0:T(8,128)}, f32[3,2,16,512]{3,2,1,0:...) custom-call(bf16[24,512]{1,0:T(8,128)(2,1)S(1)} %get-tuple-element.21.refs_0_, ...), custom_call_target="tpu_custom_call" | custom-call | tf_op jit(solution)/shard_map/hand_on/pallas_call | solution.py:446

commit v3 on v2

--- a/solution.py
+++ b/solution.py
@@ -75,7 +75,7 @@
            node, edge, recv_all, send_all, listed_at, wei, weo, wni, wno, egain, ngain, ncot, ecot,
            node_new, edge_new, node_grad, edge_grad, wgrad,
            nodes, gains, w, outgo, income, pre, normed, srows, rrows, hid, emg,
-           pool_s, pool_r, npg, ng_s, ng_r, rem_s, rem_r, ret_s, ret_r, dist_s, dist_r,
+           pool_s, pool_r, npg, ng_s, ng_r, rem_s, rem_r,
            dw, pe_s, pe_r, pn_s, pn_r, re_s, re_r, rn_s, rn_r, qe_s, qe_r, qn_s, qn_r,
            ze_s, ze_r, zn_s, zn_r, be, bn, ssem, rsem):
     g, f = lax.axis_index("region"), lax.axis_index("feat")
@@ -140,7 +140,7 @@
         w[4 + k, y, x, c] = wni[k, c]
     w[6, y, x, c] = wno[c]
     income[g] = jnp.zeros(income.shape[1:], BF16)
-    ret_r[g] = jnp.zeros(ret_r.shape[1:], BF16)
+    rem_r[g] = jnp.zeros(rem_r.shape[1:], BF16)
     recv_at = own_slice(recv_all, f, edges)
     send_at = own_slice(send_all, f, edges)
     grid = (regions, far)
@@ -172,28 +172,27 @@
         settle(w.at[pl.ds(*group), 0, pl.ds(0, SIDE - 1), 0], k)
 
         def act(part):
-            for d in range(1, SIDE):
+            for d in (2, 1, 3):
                 send(part, part, k2 + d, g, feat_at(a, lax.rem(b + d, SIDE))).start()
             send(part, part, k2, sibling, f).start()
         bundle(group, b, act)
 
-    def weights_pass(group, k2):
-        for d in range(1, SIDE):
-            settle(w.at[pl.ds(*group), 0, :, 0], k2 + d)
-            bundle(group, lax.rem(b - d + SIDE, SIDE), lambda part: send(part, part, k2, sibling, f).start())
+    def weights_pass(group, k2, d):
+        settle(w.at[pl.ds(*group), 0, :, 0], k2 + d)
+        bundle(group, lax.rem(b - d + SIDE, SIDE), lambda part: send(part, part, k2, sibling, f).start())
 
     def weights_end(group, k2):
         settle(w.at[pl.ds(*group), :, :, 0], k2)
 
+    weights_first(EDGE_W, 2)
     to_plane(lambda t: node, nodes, 0)
-    weights_first(EDGE_W, 2)
     weights_first(NODE_W, 3)
     to_plane(lambda t: gains.at[f], gains, 1)
+    weights_second(EDGE_W, 2, 5)
     settle_slots(nodes, 0)
     table = nodes[...].reshape(count, width)
     outgo[...] = mm_t(asked, table).astype(BF16).reshape(outgo.shape)
     to_line(lambda t: outgo.at[t], income, 4)
-    weights_second(EDGE_W, 2, 5)
     weights_second(NODE_W, 3, 9)
     rrows[...] = mm_t(into, table).astype(BF16)
     near_rows = mm_t(near, table)
@@ -204,7 +203,9 @@
     gain = flat(packed, lax.rem(lanes, portion) + portion * lax.div(lanes, width) == iota(shape, 0),
                 lax.div(lax.rem(iota(wide, 1), width), portion) == iota(wide, 0))
     edge_gain, node_gain = gain[:, :width], gain[:, width:]
-    weights_pass(EDGE_W, 5)
+    weights_pass(EDGE_W, 5, 1)
+    weights_pass(EDGE_W, 5, 3)
+    weights_pass(EDGE_W, 5, 2)
     settle_slots(income, 4)
     srows[...] = (near_rows + mm_t(away, income[...].reshape(far, width))).astype(BF16)
     weights_end(EDGE_W, 5)
@@ -221,13 +222,17 @@
     pool_s[...] = mm(into, fresh).astype(BF16).reshape(pool_s.shape)
     pool_r[f] = pool_s[f]
     to_plane(lambda t: pool_s.at[t], pool_r, 13)
-    weights_pass(NODE_W, 9)
+    for d in (1, 3, 2):
+        weights_pass(NODE_W, 9, d)
+    gate = sigmoid(pre[...])
+    pre[...] = gate * (1.0 + pre[...] * (1.0 - gate))
     weights_end(NODE_W, 9)
+    lat = node[...]
+    node_base = mm(lat, weight(4))
     settle_slots(pool_r, 13)
 
     pooled = jnp.sum(pool_r[...].astype(F32), axis=0).astype(BF16)
-    lat = node[...]
-    node_pre = mm(lat, weight(4)) + mm(pooled, weight(5))
+    node_pre = node_base + mm(pooled, weight(5))
     gate = sigmoid(node_pre)
     node_hid = (node_pre * gate).astype(BF16)
     node_normed, node_inverse = layer_norm(mm(node_hid, weight(6)))
@@ -238,28 +243,24 @@
     npg[f] = own_npg
     to_plane(lambda t: npg.at[f], npg, 14)
 
-    def trade(group, products, out, back, k):
-        start, n = group
-        for i in range(n):
-            dw[start + i] = products(i).reshape(dw.shape[1:])
-            out[i] = dw[start + i, :, 1 - c].astype(BF16)
-        send(out, back, k, sibling, f).start()
-
-    def along_a(group, out, back, stage, landed, k, k2):
-        start, n = group
-        settle(back, k)
+    def trade(k, product, out, back, s):
+        dw[k] = product.reshape(dw.shape[1:])
+        out[...] = dw[k, :, 1 - c].astype(BF16)
+        send(out, back, s, sibling, f).start()
+
+    def along_a(k, i, back, stage, landed, s, s2):
+        settle(back, s)
 
         def body(j, carry):
             a_, b_ = lax.div(j, SIDE), lax.rem(j, SIDE)
             at = feat_at(a_, b_)
-            for i in range(n):
-                stage[a_, i, b_] = (dw[start + i, at, c] + back[i, at].astype(F32)).astype(BF16)
+            stage[a_, i, b_] = (dw[k, at, c] + back[at].astype(F32)).astype(BF16)
             return carry
-        lax.fori_loop(0, feats, body, 0)
-        landed[a] = stage[a]
-        for d in range(1, SIDE):
+        lax.fori_loop(0, feats, body, 0, unroll=True)
+        landed[a, i] = stage[a, i]
+        for d in (2, 1, 3):
             a_ = lax.rem(a + d, SIDE)
-            send(stage.at[a_], landed.at[a], k2, g, feat_at(a_, b)).start()
+            send(stage.at[a_, i], landed.at[a, i], s2, g, feat_at(a_, b)).start()
 
     def along_b(landed, stage, landed2, k2, k3):
         settle_slots(landed, k2)
@@ -303,67 +304,47 @@
                     wgrad[start + i, c_, pl.ds(h * rows, rows)] = whole[2 * (halves * i + h) + c_].astype(F32)
 
     node_sides = ((lat, own_npg), (pooled, own_npg), (node_hid, nmg))
-    trade(NODE_W, lambda i: mm_t(*node_sides[i]), pn_s, pn_r, 15)
+    for i in range(3):
+        trade(4 + i, mm_t(*node_sides[i]), pn_s.at[i], pn_r.at[i], 29 + i)
     direct = ncot[...].astype(F32) + mm_back(own_npg, weight(4))
-    along_a(NODE_W, pn_s, pn_r, rn_s, rn_r, 15, 16)
+    for i in range(3):
+        along_a(4 + i, i, pn_r.at[i], rn_s, rn_r, 29 + i, 16)
     settle_slots(npg, 14)
 
     reached = mm_t(into, npg[...].reshape(count, width)).astype(BF16)
     total = ecot[...].astype(F32) + mm_back(reached, weight(5))
     emg[...] = layer_norm_back(total, normed[...], edge_inverse, edge_gain)
-    gate = sigmoid(pre[...])
-    slope = gate * (1.0 + pre[...] * (1.0 - gate))
-    pre_grad = (mm_back(emg[...], weight(3)) * slope).astype(BF16)
-    edge_sides = ((edge, None), (srows, None), (rrows, None), (hid, emg))
-    trade(EDGE_W, lambda i: mm_t(edge_sides[i][0][...], pre_grad if i < 3 else emg[...]), pe_s, pe_r, 17)
+    pre_grad = (mm_back(emg[...], weight(3)) * pre[...]).astype(BF16)
+    trade(3, mm_t(hid[...], emg[...]), pe_s.at[3], pe_r.at[3], 35)
     from_send = mm_back(pre_grad, weight(1)).astype(BF16)
     rem_s[...] = mm(away, from_send).astype(BF16).reshape(rem_s.shape)
-    rem_r[f] = rem_s[f]
-    to_plane(lambda t: rem_s.at[t], rem_r, 18)
+    to_line(lambda t: rem_s.at[t], rem_r, 18)
+    trade(0, mm_t(edge[...], pre_grad), pe_s.at[0], pe_r.at[0], 32)
+    along_a(3, 3, pe_r.at[3], re_s, re_r, 35, 19)
+    trade(1, mm_t(srows[...], pre_grad), pe_s.at[1], pe_r.at[1], 33)
+    along_a(0, 0, pe_r.at[0], re_s, re_r, 32, 19)
+    trade(2, mm_t(rrows[...], pre_grad), pe_s.at[2], pe_r.at[2], 34)
+    along_a(1, 1, pe_r.at[1], re_s, re_r, 33, 19)
+    along_a(2, 2, pe_r.at[2], re_s, re_r, 34, 19)
+    along_b(rn_r, qn_s, qn_r, 16, 20)
     from_recv = mm_back(pre_grad, weight(2)).astype(BF16)
-    ng_s[...] = (mm(near, from_send) + mm(into, from_recv)).astype(BF16).reshape(ng_s.shape)
+    ng = mm(near, from_send) + mm(into, from_recv)
+    edge_grad[...] = total + mm_back(pre_grad, weight(0))
+    along_b(re_r, qe_s, qe_r, 19, 24)
+
+    settle_slots(rem_r, 18)
+    ng = ng + mm(asked, rem_r[...].reshape(far, width))
+    ng_s[...] = ng.astype(BF16).reshape(ng_s.shape)
     ng_r[f] = ng_s[f]
-    edge_grad[...] = total + mm_back(pre_grad, weight(0))
-    along_a(EDGE_W, pe_s, pe_r, re_s, re_r, 17, 19)
-    along_b(rn_r, qn_s, qn_r, 16, 20)
+    along_z(qn_r, zn_s, zn_r, 20, 23)
+    along_z(qe_r, ze_s, ze_r, 24, 26)
     to_plane(lambda t: ng_s.at[t], ng_r, 21)
-
-    settle_slots(rem_r, 18)
-    ret_s[...] = jnp.sum(rem_r[...].astype(F32), axis=0).astype(BF16)
-
-    @pl.when(g != f)
-    def _():
-        send(ret_s, ret_r.at[g], 22, f, f).start()
-
-    along_z(qn_r, zn_s, zn_r, 20, 23)
-    along_b(re_r, qe_s, qe_r, 19, 24)
-
-    @pl.when(g == f)
-    def _():
-        send(ret_r.at[pl.ds(0, regions - 1)], ret_r.at[pl.ds(0, regions - 1)], 22, g, f).wait_recv()
-        dist_s[...] = mm(asked, ret_r[...].reshape(far, width)).astype(BF16).reshape(dist_s.shape)
-        dist_r[...] = dist_s[f]
-        for d in range(1, feats):
-            t = lax.rem(f + d, feats)
-            send(dist_s.at[t], dist_r, 25, g, t).start()
-
-    along_z(qe_r, ze_s, ze_r, 24, 26)
     to_all(zn_r, bn, 23, 27, scales[1])
     to_all(ze_r, be, 26, 28, scales[0])
     settle_slots(ng_r, 21)
-
-    @pl.when(g != f)
-    def _():
-        send(ret_s, ret_s, 22, f, f).wait_send()
-        send(dist_r, dist_r, 25, g, f).wait_recv()
-
-    node_grad[...] = direct + jnp.sum(ng_r[...].astype(F32), axis=0) + dist_r[...].astype(F32)
+    node_grad[...] = direct + jnp.sum(ng_r[...].astype(F32), axis=0)
     finish(NODE_W, bn, 27)
     finish(EDGE_W, be, 28)
-
-    @pl.when(g == f)
-    def _():
-        send(dist_s.at[pl.ds(0, feats - 1)], dist_s.at[pl.ds(0, feats - 1)], 25, g, f).wait_send()
 
 
 def hand_on(*refs):
@@ -404,14 +385,13 @@
         *pair(F32, edges, width),
         *[v(BF16, edges, width)] * 4,
         *pair(BF16, *nodes_like), v(BF16, *nodes_like), *pair(BF16, *nodes_like), *pair(BF16, *line_like),
-        v(BF16, slots, width), v(BF16, *line_like), v(BF16, *nodes_like), v(BF16, per, width),
         v(F32, ne + nn, feats, 2, part, width),
         *pair(BF16, ne, feats, part, width), *pair(BF16, nn, feats, part, width),
         *pair(BF16, SIDE, ne, SIDE, part, width), *pair(BF16, SIDE, nn, SIDE, part, width),
         *pair(BF16, SIDE, ne, part, width), *pair(BF16, SIDE, nn, part, width),
         *pair(BF16, regions // 2, piece, width), *pair(BF16, regions // 2, piece, width),
         *pair(BF16, regions, piece, width),
-        pltpu.SemaphoreType.DMA((29,)), pltpu.SemaphoreType.DMA((29,)),
+        pltpu.SemaphoreType.DMA((36,)), pltpu.SemaphoreType.DMA((36,)),
     ]
 
     args = (node_lat, edge_lat, receiver_row.reshape(lines), sender_slot.reshape(lines), send_rows,

time: 82.9 us -> 75.9 us (0.916)
  Pallas kernels: 82.1 us -> 75.1 us
    pallas_call x1, Pallas kernels: 81.1 us -> 74.1 us  [shards(): pl.pallas_call(body, name='layer', out_shape=[jax.ShapeDtypeStruct(*k) fo...]
where the time goes in v3:
time: 75.9 us; the launch traced here: 75.8 us
  Pallas kernels  75.1 us (99%)
    pallas_call x1, Pallas kernels, shards(): pl.pallas_call(body, name='layer', out_shape=[jax.ShapeDtypeStruct(*k) fo...  74.1 us

profile of v3, /device:TPU:1, one launch (start us, length us, event | category | flops | bytes accessed | tf_op | source)
XLA Modules:
  0.0 75.8 jit_solution(2017707143090852371)
XLA Ops:
  0.6 74.1 %layer.1 = (bf16[24,512]{1,0:T(8,128)(2,1)S(1)}, bf16[192,512]{1,0:T(8,128)(2,1)S(1)}, f32[24,512]{1,0:T(8,128)S(1)}, f32[192,512]{1,0:T(8,128)S(1)}, f32[7,2,16,512]{3,2,1,0:T(8,128)S(1)}) custom-call(bf16[24,512]{1,0:T(8,128)(2,1)} %refs_0_.1, bf16[192,512]{1,0:T(8,128)(2,1)} %refs_1_.1, s32[24,1,128]{2,1,0:T(1,128)} %bitcast.16, s32[24,1,128]{2,1,0:T(1,128)} %bitcast.17, ...), custom_call_target="tpu_custom_call" | custom-call | tf_op jit(solution)/shard_map/layer/pallas_call | solution.py:415
  74.7 1.1 %hand_on.1 = (bf16[24,512]{1,0:T(8,128)(2,1)}, bf16[192,512]{1,0:T(8,128)(2,1)}, f32[24,512]{1,0:T(8,128)}, f32[192,512]{1,0:T(8,128)}, f32[3,2,16,512]{3,2,1,0:...) custom-call(bf16[24,512]{1,0:T(8,128)(2,1)S(1)} %get-tuple-element.21.refs_0_, ...), custom_call_target="tpu_custom_call" | custom-call | tf_op jit(solution)/shard_map/hand_on/pallas_call | solution.py:426

commit v4 on v3

--- a/solution.py
+++ b/solution.py
@@ -11,6 +11,18 @@
 SIDE = 4
 EDGE_W, NODE_W = (0, 4), (4, 3)
 VMEM_LIMIT = 44 * 2**20
+
+
+def hops(d, n):
+    return min(d, n - d)
+
+
+def far_first(n):
+    return sorted(range(1, n), key=lambda d: -hops(d, n))
+
+
+PLANE_STEPS = sorted(((dy, dx) for dy in range(SIDE) for dx in range(SIDE) if dy or dx),
+                     key=lambda s: -hops(s[0], SIDE) - hops(s[1], SIDE))
 
 
 def dot(a, b, da, db):
@@ -101,18 +113,14 @@
             device_id=(region, feat), device_id_type=MESH)
 
     def to_plane(src_of, dst, k):
-        def body(j, carry):
-            t = lax.rem(f + j, feats)
+        for dy, dx in PLANE_STEPS:
+            t = SIDE * lax.rem(y + dy, SIDE) + lax.rem(x + dx, SIDE)
             send(src_of(t), dst.at[f], k, g, t).start()
-            return carry
-        lax.fori_loop(1, feats, body, 0)
 
     def to_line(src_of, dst, k):
-        def body(j, carry):
+        for j in far_first(regions):
             t = lax.rem(g + j, regions)
             send(src_of(t), dst.at[g], k, t, f).start()
-            return carry
-        lax.fori_loop(1, regions, body, 0)
 
     def settle(view, k):
         send(view, view, k, g, f).wait()
@@ -122,17 +130,16 @@
 
     barrier = pltpu.get_barrier_semaphore()
 
-    def greet(j, carry):
-        pl.semaphore_signal(barrier, inc=1, device_id=(g, lax.rem(f + j, feats)), device_id_type=MESH)
+    for (dy, dx), j in zip(PLANE_STEPS, far_first(regions)):
+        t = SIDE * lax.rem(y + dy, SIDE) + lax.rem(x + dx, SIDE)
+        pl.semaphore_signal(barrier, inc=1, device_id=(g, t), device_id_type=MESH)
         pl.semaphore_signal(barrier, inc=1, device_id=(lax.rem(g + j, regions), f), device_id_type=MESH)
-        return carry
-    lax.fori_loop(1, feats, greet, 0)
     for fetch in fetches:
         fetch.wait()
 
     portion = egain.shape[1]
     gains[f] = jnp.concatenate([egain[...], ngain[...], jnp.zeros((1, gains.shape[2] - 2 * portion), F32)], axis=1)
-    nodes[f] = node[...]
+    nodes[y, x] = node[...]
     for k in range(3):
         w[k, y, x, c] = wei[k, c]
     w[3, y, x, c] = weo[c]
@@ -172,28 +179,49 @@
         settle(w.at[pl.ds(*group), 0, pl.ds(0, SIDE - 1), 0], k)
 
         def act(part):
-            for d in (2, 1, 3):
+            for d in (1, 3):
                 send(part, part, k2 + d, g, feat_at(a, lax.rem(b + d, SIDE))).start()
             send(part, part, k2, sibling, f).start()
         bundle(group, b, act)
 
     def weights_pass(group, k2, d):
         settle(w.at[pl.ds(*group), 0, :, 0], k2 + d)
-        bundle(group, lax.rem(b - d + SIDE, SIDE), lambda part: send(part, part, k2, sibling, f).start())
+
+        def act(part):
+            send(part, part, k2, sibling, f).start()
+            if d != 2:
+                half = part.at[:, :, pl.ds(0 if d == 1 else part.shape[2] // 2, part.shape[2] // 2)]
+                send(half, half, k2 + 2, g, feat_at(a, lax.rem(b + d, SIDE))).start()
+        bundle(group, lax.rem(b - d + SIDE, SIDE), act)
 
     def weights_end(group, k2):
         settle(w.at[pl.ds(*group), :, :, 0], k2)
 
+    def nodes_second(part):
+        for d in (2, 1, 3):
+            send(part, part, 36, g, feat_at(a, lax.rem(b + d, SIDE))).start()
+
+    for d in range(1, SIDE):
+        send(node, nodes.at[y, x], 0, g, feat_at(lax.rem(a + d, SIDE), b)).start()
     weights_first(EDGE_W, 2)
-    to_plane(lambda t: node, nodes, 0)
     weights_first(NODE_W, 3)
     to_plane(lambda t: gains.at[f], gains, 1)
+    settle(nodes.at[0, pl.ds(0, SIDE - 1)], 0)
+
+    @pl.when(first)
+    def _():
+        nodes_second(nodes.at[y])
+
+    @pl.when(c == 1)
+    def _():
+        nodes_second(nodes.at[:, x])
+
     weights_second(EDGE_W, 2, 5)
-    settle_slots(nodes, 0)
+    weights_second(NODE_W, 3, 9)
+    settle_slots(nodes, 36)
     table = nodes[...].reshape(count, width)
     outgo[...] = mm_t(asked, table).astype(BF16).reshape(outgo.shape)
     to_line(lambda t: outgo.at[t], income, 4)
-    weights_second(NODE_W, 3, 9)
     rrows[...] = mm_t(into, table).astype(BF16)
     near_rows = mm_t(near, table)
     settle_slots(gains, 1)
@@ -203,9 +231,10 @@
     gain = flat(packed, lax.rem(lanes, portion) + portion * lax.div(lanes, width) == iota(shape, 0),
                 lax.div(lax.rem(iota(wide, 1), width), portion) == iota(wide, 0))
     edge_gain, node_gain = gain[:, :width], gain[:, width:]
-    weights_pass(EDGE_W, 5, 1)
-    weights_pass(EDGE_W, 5, 3)
-    weights_pass(EDGE_W, 5, 2)
+    for d in (1, 3, 2):
+        weights_pass(EDGE_W, 5, d)
+    weights_pass(NODE_W, 9, 1)
+    weights_pass(NODE_W, 9, 3)
     settle_slots(income, 4)
     srows[...] = (near_rows + mm_t(away, income[...].reshape(far, width))).astype(BF16)
     weights_end(EDGE_W, 5)
@@ -222,8 +251,7 @@
     pool_s[...] = mm(into, fresh).astype(BF16).reshape(pool_s.shape)
     pool_r[f] = pool_s[f]
     to_plane(lambda t: pool_s.at[t], pool_r, 13)
-    for d in (1, 3, 2):
-        weights_pass(NODE_W, 9, d)
+    weights_pass(NODE_W, 9, 2)
     gate = sigmoid(pre[...])
     pre[...] = gate * (1.0 + pre[...] * (1.0 - gate))
     weights_end(NODE_W, 9)
@@ -284,7 +312,7 @@
             stage[pl.ds(pieces.shape[0], chips - pieces.shape[0])] = jnp.zeros(
                 (chips - pieces.shape[0], rows, width), BF16)
         landed2[z] = stage[z]
-        for d in range(1, chips):
+        for d in far_first(chips):
             z_ = lax.rem(z + d, chips)
             send(stage.at[z_], landed2.at[z], k4, 2 * z_ + c, f).start()
 
@@ -380,7 +408,7 @@
         return [v(dtype, *shape)] * 2
 
     scratch = [
-        v(BF16, *nodes_like), v(F32, feats, 1, 128), v(BF16, ne + nn, SIDE, SIDE, 2, part, width),
+        v(BF16, SIDE, SIDE, per, width), v(F32, feats, 1, 128), v(BF16, ne + nn, SIDE, SIDE, 2, part, width),
         *pair(BF16, *line_like),
         *pair(F32, edges, width),
         *[v(BF16, edges, width)] * 4,
@@ -391,7 +419,7 @@
         *pair(BF16, SIDE, ne, part, width), *pair(BF16, SIDE, nn, part, width),
         *pair(BF16, regions // 2, piece, width), *pair(BF16, regions // 2, piece, width),
         *pair(BF16, regions, piece, width),
-        pltpu.SemaphoreType.DMA((36,)), pltpu.SemaphoreType.DMA((36,)),
+        pltpu.SemaphoreType.DMA((37,)), pltpu.SemaphoreType.DMA((37,)),
     ]
 
     args = (node_lat, edge_lat, receiver_row.reshape(lines), sender_slot.reshape(lines), send_rows,

time: 75.9 us -> 73.5 us (0.968)
  Pallas kernels: 75.1 us -> 72.8 us
    pallas_call x1, Pallas kernels: 74.1 us -> 71.7 us  [shards(): pl.pallas_call(body, name='layer', out_shape=[jax.ShapeDtypeStruct(*k) fo...]
where the time goes in v4:
time: 73.5 us; the launch traced here: 73.4 us
  Pallas kernels  72.8 us (99%)
    pallas_call x1, Pallas kernels, shards(): pl.pallas_call(body, name='layer', out_shape=[jax.ShapeDtypeStruct(*k) fo...  71.7 us

profile of v4, /device:TPU:1, one launch (start us, length us, event | category | flops | bytes accessed | tf_op | source)
XLA Modules:
  0.0 73.4 jit_solution(7591071524454486644)
XLA Ops:
  0.6 71.7 %layer.1 = (bf16[24,512]{1,0:T(8,128)(2,1)S(1)}, bf16[192,512]{1,0:T(8,128)(2,1)S(1)}, f32[24,512]{1,0:T(8,128)S(1)}, f32[192,512]{1,0:T(8,128)S(1)}, f32[7,2,16,512]{3,2,1,0:T(8,128)S(1)}) custom-call(bf16[24,512]{1,0:T(8,128)(2,1)} %refs_0_.1, bf16[192,512]{1,0:T(8,128)(2,1)} %refs_1_.1, s32[24,1,128]{2,1,0:T(1,128)} %bitcast.16, s32[24,1,128]{2,1,0:T(1,128)} %bitcast.17, ...), custom_call_target="tpu_custom_call" | custom-call | tf_op jit(solution)/shard_map/layer/pallas_call | solution.py:443
  72.4 1.1 %hand_on.1 = (bf16[24,512]{1,0:T(8,128)(2,1)}, bf16[192,512]{1,0:T(8,128)(2,1)}, f32[24,512]{1,0:T(8,128)}, f32[192,512]{1,0:T(8,128)}, f32[3,2,16,512]{3,2,1,0:...) custom-call(bf16[24,512]{1,0:T(8,128)(2,1)S(1)} %get-tuple-element.21.refs_0_, ...), custom_call_target="tpu_custom_call" | custom-call | tf_op jit(solution)/shard_map/hand_on/pallas_call | solution.py:454

commit v5 on v3

--- a/solution.py
+++ b/solution.py
@@ -11,6 +11,18 @@
 SIDE = 4
 EDGE_W, NODE_W = (0, 4), (4, 3)
 VMEM_LIMIT = 44 * 2**20
+
+
+def hops(d, n):
+    return min(d, n - d)
+
+
+def far_first(n):
+    return sorted(range(1, n), key=lambda d: -hops(d, n))
+
+
+PLANE_STEPS = sorted(((dy, dx) for dy in range(SIDE) for dx in range(SIDE) if dy or dx),
+                     key=lambda s: -hops(s[0], SIDE) - hops(s[1], SIDE))
 
 
 def dot(a, b, da, db):
@@ -101,18 +113,14 @@
             device_id=(region, feat), device_id_type=MESH)
 
     def to_plane(src_of, dst, k):
-        def body(j, carry):
-            t = lax.rem(f + j, feats)
+        for dy, dx in PLANE_STEPS:
+            t = SIDE * lax.rem(y + dy, SIDE) + lax.rem(x + dx, SIDE)
             send(src_of(t), dst.at[f], k, g, t).start()
-            return carry
-        lax.fori_loop(1, feats, body, 0)
 
     def to_line(src_of, dst, k):
-        def body(j, carry):
+        for j in far_first(regions):
             t = lax.rem(g + j, regions)
             send(src_of(t), dst.at[g], k, t, f).start()
-            return carry
-        lax.fori_loop(1, regions, body, 0)
 
     def settle(view, k):
         send(view, view, k, g, f).wait()
@@ -122,11 +130,10 @@
 
     barrier = pltpu.get_barrier_semaphore()
 
-    def greet(j, carry):
-        pl.semaphore_signal(barrier, inc=1, device_id=(g, lax.rem(f + j, feats)), device_id_type=MESH)
+    for (dy, dx), j in zip(PLANE_STEPS, far_first(regions)):
+        t = SIDE * lax.rem(y + dy, SIDE) + lax.rem(x + dx, SIDE)
+        pl.semaphore_signal(barrier, inc=1, device_id=(g, t), device_id_type=MESH)
         pl.semaphore_signal(barrier, inc=1, device_id=(lax.rem(g + j, regions), f), device_id_type=MESH)
-        return carry
-    lax.fori_loop(1, feats, greet, 0)
     for fetch in fetches:
         fetch.wait()
 
@@ -154,7 +161,7 @@
 
     def weights_first(group, k):
         part = w.at[pl.ds(*group), y, x, c]
-        for d in range(1, SIDE):
+        for d in (2, 1, 3):
             send(part, part, k, g, feat_at(lax.rem(a + d, SIDE), b)).start()
 
     def bundle(group, b_, act):
@@ -270,7 +277,7 @@
             return carry
         lax.fori_loop(0, SIDE, body, 0)
         landed2[b] = stage[b]
-        for d in range(1, SIDE):
+        for d in (2, 1, 3):
             b_ = lax.rem(b + d, SIDE)
             send(stage.at[b_], landed2.at[b], k3, g, feat_at(a, b_)).start()
 
@@ -284,7 +291,7 @@
             stage[pl.ds(pieces.shape[0], chips - pieces.shape[0])] = jnp.zeros(
                 (chips - pieces.shape[0], rows, width), BF16)
         landed2[z] = stage[z]
-        for d in range(1, chips):
+        for d in far_first(chips):
             z_ = lax.rem(z + d, chips)
             send(stage.at[z_], landed2.at[z], k4, 2 * z_ + c, f).start()
 

time: 75.9 us -> 73 us (0.962)
  Pallas kernels: 75.1 us -> 72.2 us
    pallas_call x1, Pallas kernels: 74.1 us -> 71.2 us  [shards(): pl.pallas_call(body, name='layer', out_shape=[jax.ShapeDtypeStruct(*k) fo...]
where the time goes in v5:
time: 73 us; the launch traced here: 72.9 us
  Pallas kernels  72.2 us (99%)
    pallas_call x1, Pallas kernels, shards(): pl.pallas_call(body, name='layer', out_shape=[jax.ShapeDtypeStruct(*k) fo...  71.2 us

profile of v5, /device:TPU:1, one launch (start us, length us, event | category | flops | bytes accessed | tf_op | source)
XLA Modules:
  0.0 72.9 jit_solution(15595465118507915679)
XLA Ops:
  0.6 71.2 %layer.1 = (bf16[24,512]{1,0:T(8,128)(2,1)S(1)}, bf16[192,512]{1,0:T(8,128)(2,1)S(1)}, f32[24,512]{1,0:T(8,128)S(1)}, f32[192,512]{1,0:T(8,128)S(1)}, f32[7,2,16,512]{3,2,1,0:T(8,128)S(1)}) custom-call(bf16[24,512]{1,0:T(8,128)(2,1)} %refs_0_.1, bf16[192,512]{1,0:T(8,128)(2,1)} %refs_1_.1, s32[24,1,128]{2,1,0:T(1,128)} %bitcast.16, s32[24,1,128]{2,1,0:T(1,128)} %bitcast.17, ...), custom_call_target="tpu_custom_call" | custom-call | tf_op jit(solution)/shard_map/layer/pallas_call | solution.py:422
  71.8 1.1 %hand_on.1 = (bf16[24,512]{1,0:T(8,128)(2,1)}, bf16[192,512]{1,0:T(8,128)(2,1)}, f32[24,512]{1,0:T(8,128)}, f32[192,512]{1,0:T(8,128)}, f32[3,2,16,512]{3,2,1,0:...) custom-call(bf16[24,512]{1,0:T(8,128)(2,1)S(1)} %get-tuple-element.21.refs_0_, ...), custom_call_target="tpu_custom_call" | custom-call | tf_op jit(solution)/shard_map/hand_on/pallas_call | solution.py:433
